TPU v7x, 768 devices: a whole 4x8x12 slice. The times are simulated.
768 devices in a mesh: gx: 96 (over y, x, z_lo), gy: 8 (over z_hi, core).
Axes of the slice: x: 4, y: 8, z: 12 (z_hi: 4, z_lo: 3; z = z_hi * 3 + z_lo), core: 2. Of those that a mesh axis runs over, the one named last changes fastest.
Arguments:
- phase_pops: float32 [15, 192, 16, 1024], P(None, 'gx', None, 'gy'), may hold values from 0 to 0.1
- flow_pops: float32 [19, 192, 16, 1024], P(None, 'gx', None, 'gy'), may hold values from 0 to 0.1
- solid_flags: int32 [192, 16, 1024], P('gx', None, 'gy'), may hold values 0 or 1
Outputs:
- phase_out: float32 [15, 192, 16, 1024], P(None, 'gx', None, 'gy')
- flow_out: float32 [19, 192, 16, 1024], P(None, 'gx', None, 'gy')
All inputs are finite; a program needn't handle non-finite values. No bound on the sum of `solid_flags` on one device may be relied on, other than what follows from the above.
Results may differ from a plain program's by a relative error of at most 0.0001.
Values sent between devices are 32-bit elements; how exact they have to be, the bound alone decides.
No kernel may reach another device: no remote copies, remote signals or barrier semaphores. Data moves between devices by JAX's collectives and lax.ppermute only.
A program may use at most 32 MiB of HBM per device.

v0:
```python
import jax
import jax.numpy as jnp
from jax import lax
from jax.sharding import PartitionSpec as P

STEPS = 2


PHASE_VELOCITIES = [
    (0, 0, 0),
    (1, 0, 0),
    (-1, 0, 0),
    (0, 1, 0),
    (0, -1, 0),
    (0, 0, 1),
    (0, 0, -1),
    (1, 1, 1),
    (1, 1, -1),
    (1, -1, 1),
    (1, -1, -1),
    (-1, 1, 1),
    (-1, 1, -1),
    (-1, -1, 1),
    (-1, -1, -1),
]
PHASE_WEIGHTS = [2.0 / 9.0] + [1.0 / 9.0] * 6 + [1.0 / 72.0] * 8
FLOW_VELOCITIES = [
    (0, 0, 0),
    (1, 0, 0),
    (-1, 0, 0),
    (0, 1, 0),
    (0, -1, 0),
    (0, 0, 1),
    (0, 0, -1),
    (1, 1, 0),
    (1, -1, 0),
    (-1, 1, 0),
    (-1, -1, 0),
    (1, 0, 1),
    (1, 0, -1),
    (-1, 0, 1),
    (-1, 0, -1),
    (0, 1, 1),
    (0, 1, -1),
    (0, -1, 1),
    (0, -1, -1),
]
FLOW_WEIGHTS = [1.0 / 3.0] + [1.0 / 18.0] * 6 + [1.0 / 36.0] * 12
SURFACE_TENSION = 0.05
INTERFACE_WIDTH = 4.0
GRADIENT_FLOOR = 0.1
PHASE_LAMBDA = 0.3
PHASE_RELAX = 0.8
PHASE_FORWARD = [number for number in range(15) if PHASE_VELOCITIES[number][0] == 1]
PHASE_BACKWARD = [number for number in range(15) if PHASE_VELOCITIES[number][0] == -1]
PHASE_UPWARD = [number for number in range(15) if PHASE_VELOCITIES[number][1] == 1]
PHASE_DOWNWARD = [number for number in range(15) if PHASE_VELOCITIES[number][1] == -1]
PACKED_FORWARD = [0] + [number + 1 for number in range(19) if FLOW_VELOCITIES[number][0] == 1]
PACKED_BACKWARD = [0] + [number + 1 for number in range(19) if FLOW_VELOCITIES[number][0] == -1]
PACKED_UPWARD = [0] + [number + 1 for number in range(19) if FLOW_VELOCITIES[number][1] == 1]
PACKED_DOWNWARD = [0] + [number + 1 for number in range(19) if FLOW_VELOCITIES[number][1] == -1]


def shifted(block, axis, distance):
    devices = range(lax.axis_size(axis))
    route = [((i - distance) % len(devices), i) for i in devices]
    return lax.ppermute(block, axis, route)


def reverse_of(velocities):
    return [velocities.index((-vector[0], -vector[1], -vector[2])) for vector in velocities]


def relax(phase_read, flow_read, phase_field, neighbours, solid_cells):
    gradient = []
    for coordinate in range(3):
        total = jnp.zeros_like(phase_field)
        for number in range(19):
            if FLOW_VELOCITIES[number][coordinate] != 0:
                total = (
                    total
                    + FLOW_WEIGHTS[number]
                    * FLOW_VELOCITIES[number][coordinate]
                    * neighbours[number]
                )
        gradient.append(3.0 * total)
    laplacian = jnp.zeros_like(phase_field)
    for number in range(1, 19):
        laplacian = laplacian + FLOW_WEIGHTS[number] * (neighbours[number] - phase_field)
    laplacian = 6.0 * laplacian
    magnitude = jnp.sqrt(gradient[0] ** 2 + gradient[1] ** 2 + gradient[2] ** 2)
    scaling = 1.0 / jnp.maximum(magnitude, GRADIENT_FLOOR)
    normal = [component * scaling for component in gradient]
    clipped = jnp.clip(phase_field, 0.0, 1.0)
    density = 1.0 + 2.0 * clipped
    relax_time = 0.6 + 0.4 * clipped
    beta_value = 12.0 * SURFACE_TENSION / INTERFACE_WIDTH
    kappa_value = 1.5 * SURFACE_TENSION * INTERFACE_WIDTH
    potential = (
        4.0 * beta_value * phase_field * (phase_field - 1.0) * (phase_field - 0.5)
        - kappa_value * laplacian
    )
    force_terms = [potential * component for component in gradient]
    pressure = jnp.sum(flow_read, axis=0)
    velocity = []
    for coordinate in range(3):
        moment = 0.5 * force_terms[coordinate]
        for number in range(19):
            if FLOW_VELOCITIES[number][coordinate] != 0:
                moment = moment + FLOW_VELOCITIES[number][coordinate] * flow_read[number]
        velocity.append(moment / density)
    speed_sq = velocity[0] ** 2 + velocity[1] ** 2 + velocity[2] ** 2
    force_factor = 3.0 * (1.0 - 0.5 / relax_time) / density
    flow_reverse = reverse_of(FLOW_VELOCITIES)
    flow_post = []
    for number in range(19):
        vector = FLOW_VELOCITIES[number]
        weight = FLOW_WEIGHTS[number]
        along = vector[0] * velocity[0] + vector[1] * velocity[1] + vector[2] * velocity[2]
        along_force = (
            vector[0] * force_terms[0] + vector[1] * force_terms[1] + vector[2] * force_terms[2]
        )
        equilibrium = weight * (pressure + 3.0 * along + 4.5 * along * along - 1.5 * speed_sq)
        current = flow_read[number]
        post_value = (
            current - (current - equilibrium) / relax_time + weight * force_factor * along_force
        )
        flow_post.append(jnp.where(solid_cells, flow_read[flow_reverse[number]], post_value))
    phase_reverse = reverse_of(PHASE_VELOCITIES)
    interface = PHASE_LAMBDA * phase_field * (1.0 - phase_field)
    phase_post = []
    for number in range(15):
        vector = PHASE_VELOCITIES[number]
        weight = PHASE_WEIGHTS[number]
        along = vector[0] * velocity[0] + vector[1] * velocity[1] + vector[2] * velocity[2]
        along_normal = vector[0] * normal[0] + vector[1] * normal[1] + vector[2] * normal[2]
        equilibrium = weight * (phase_field * (1.0 + 3.0 * along) + interface * along_normal)
        current = phase_read[number]
        post_value = current - (current - equilibrium) / PHASE_RELAX
        phase_post.append(jnp.where(solid_cells, phase_read[phase_reverse[number]], post_value))
    return (jnp.stack(phase_post), jnp.stack(flow_post))


def place_layers(lateral, forward_rows, backward_rows, ahead_rows, behind):
    empty_layer = jnp.zeros_like(lateral[:, :1])
    left_layer = empty_layer.at[jnp.array(forward_rows)].set(ahead_rows)
    right_layer = empty_layer.at[jnp.array(backward_rows)].set(behind)
    return jnp.concatenate([left_layer, lateral, right_layer], axis=1)


def with_rims(stacked, forward_rows, backward_rows, upward_rows, downward_rows):
    upper = shifted(stacked[jnp.array(upward_rows), :, :, -1:], "gy", 1)
    lower = shifted(stacked[jnp.array(downward_rows), :, :, :1], "gy", -1)
    empty_column = jnp.zeros_like(stacked[:, :, :, :1])
    left_column = empty_column.at[jnp.array(upward_rows)].set(upper)
    right_column = empty_column.at[jnp.array(downward_rows)].set(lower)
    lateral = jnp.concatenate([left_column, stacked, right_column], axis=3)
    ahead_rows = shifted(lateral[jnp.array(forward_rows), -1:], "gx", 1)
    behind = shifted(lateral[jnp.array(backward_rows), :1], "gx", -1)
    return place_layers(lateral, forward_rows, backward_rows, ahead_rows, behind)


def pull_plane(component, vector, width_x, width_y):
    window = component[
        1 - vector[0] : 1 - vector[0] + width_x, :, 1 - vector[1] : 1 - vector[1] + width_y
    ]
    return jnp.roll(window, vector[2], axis=1)


def shards(phase_pops, flow_pops, solid_flags):
    solid_cells = solid_flags > 0
    width_x = phase_pops.shape[1]
    width_y = phase_pops.shape[3]
    for step in range(STEPS):
        padded = with_rims(phase_pops, PHASE_FORWARD, PHASE_BACKWARD, PHASE_UPWARD, PHASE_DOWNWARD)
        phase_read = jnp.stack(
            [
                pull_plane(padded[number], PHASE_VELOCITIES[number], width_x, width_y)
                for number in range(15)
            ]
        )
        phase_field = jnp.sum(phase_read, axis=0)
        packed = with_rims(
            jnp.concatenate([phase_field[None], flow_pops], axis=0),
            PACKED_FORWARD,
            PACKED_BACKWARD,
            PACKED_UPWARD,
            PACKED_DOWNWARD,
        )
        flow_read = jnp.stack(
            [
                pull_plane(packed[number + 1], FLOW_VELOCITIES[number], width_x, width_y)
                for number in range(19)
            ]
        )
        neighbours = [
            pull_plane(packed[0], (-vector[0], -vector[1], -vector[2]), width_x, width_y)
            for vector in FLOW_VELOCITIES
        ]
        phase_pops, flow_pops = relax(phase_read, flow_read, phase_field, neighbours, solid_cells)
    return (phase_pops, flow_pops)


def solution(mesh):
    placed = (P(None, "gx", None, "gy"), P(None, "gx", None, "gy"), P("gx", None, "gy"))
    return jax.shard_map(
        shards,
        mesh=mesh,
        in_specs=placed,
        out_specs=(P(None, "gx", None, "gy"), P(None, "gx", None, "gy")),
        check_vma=False,
    )
```

profile of v0, /device:TPU:1, one launch (start us, length us, event | category | flops | bytes accessed | tf_op | source)
XLA Modules:
  0.0 154.8 jit_solution(3805198256993767675)
XLA Ops:
  0.7 2.5 %copy.141 = f32[15,2,16,128]{2,1,3,0:T(2,128)S(1)} copy(f32[15,2,16,128]{3,2,1,0:T(8,128)} %param.35) | data formatting | bytes 491520 | tf_op args[0]
  3.8 9.0 %collective-permute-start = (f32[5,2,16,1]{2,1,0,3:T(2,128)S(1)}, f32[5,2,16,1]{2,1,0,3:T(2,128)S(1)}, u32[]{:S(2)}, u32[]{:S(2)}) collective-permute-start(f32[5,2,16,1]{2,1,0,3:T(2,128)S(1)} %bitcast.381), channel_id=1, source_target_pairs={{7,0},{0,1},{1,2},{2,3},{3,4},{4,5},{5,6},{6,7},{15,8},{8,9},{9,10... | collective-permute-start | bytes 1928 | tf_op jit(solution)/shard_map/ppermute | solution.py:67
  13.4 5.3 %collective-permute-start.1 = (f32[5,2,16,1]{2,1,0,3:T(2,128)S(1)}, f32[5,2,16,1]{2,1,0,3:T(2,128)S(1)}, u32[]{:S(2)}, u32[]{:S(2)}) collective-permute-start(f32[5,2,16,1]{2,1,0,3:T(2,128)S(1)} %bitcast.379), channel_id=1, source_target_pairs={{1,0},{2,1},{3,2},{4,3},{5,4},{6,5},{7,6},{0,7},{9,8},{10,9},{11,1... | collective-permute-start | bytes 1928 | tf_op jit(solution)/shard_map/ppermute | solution.py:67
  21.9 13.3 %collective-permute-start.3 = (f32[5,1,16,130]{3,2,0,1:T(8,128)S(1)}, f32[5,1,16,130]{3,2,0,1:T(8,128)S(1)}, u32[]{:S(2)}, u32[]{:S(2)}) collective-permute-start(f32[5,1,16,130]{3,2,0,1:T(8,128)S(1)} %bitcast.365), channel_id=1, source_target_pairs={{8,0},{16,8},{24,16},{32,24},{40,32},{48,40},{56,48},{64,56},{72,6... | collective-permute-start | bytes 124808 | tf_op jit(solution)/shard_map/ppermute | solution.py:67
  35.9 1.9 %collective-permute-start.2 = (f32[5,1,16,130]{3,2,0,1:T(8,128)S(1)}, f32[5,1,16,130]{3,2,0,1:T(8,128)S(1)}, u32[]{:S(2)}, u32[]{:S(2)}) collective-permute-start(f32[5,1,16,130]{3,2,0,1:T(8,128)S(1)} %bitcast.363), channel_id=1, source_target_pairs={{760,0},{0,8},{8,16},{16,24},{24,32},{32,40},{40,48},{48,56},{56,6... | collective-permute-start | bytes 124808 | tf_op jit(solution)/shard_map/ppermute | solution.py:67
  38.6 8.0 %collective-permute-done.2 = f32[5,1,16,130]{3,2,0,1:T(8,128)S(1)} collective-permute-done((f32[5,1,16,130]{3,2,0,1:T(8,128)S(1)}, f32[5,1,16,130]{3,2,0,1:T(8,128)S(1)}, u32[]{:S(2)}, u32[]{:S(2)}) %collective-permute-start.2) | collective-permute-done | bytes 41632 | tf_op jit(solution)/shard_map/ppermute | solution.py:67
  49.4 1.3 copy.146
  51.3 4.2 %collective-permute-start.4 = (f32[6,2,16,1]{2,1,0,3:T(2,128)S(1)}, f32[6,2,16,1]{2,1,0,3:T(2,128)S(1)}, u32[]{:S(2)}, u32[]{:S(2)}) collective-permute-start(f32[6,2,16,1]{2,1,0,3:T(2,128)S(1)} %bitcast.377), channel_id=1, source_target_pairs={{7,0},{0,1},{1,2},{2,3},{3,4},{4,5},{5,6},{6,7},{15,8},{8,9},{9,10... | collective-permute-start | bytes 2312 | tf_op jit(solution)/shard_map/ppermute | solution.py:67
  56.1 1.9 %collective-permute-start.5 = (f32[6,2,16,1]{2,1,0,3:T(2,128)S(1)}, f32[6,2,16,1]{2,1,0,3:T(2,128)S(1)}, u32[]{:S(2)}, u32[]{:S(2)}) collective-permute-start(f32[6,2,16,1]{2,1,0,3:T(2,128)S(1)} %bitcast.373), channel_id=1, source_target_pairs={{1,0},{2,1},{3,2},{4,3},{5,4},{6,5},{7,6},{0,7},{9,8},{10,9},{11,1... | collective-permute-start | bytes 2312 | tf_op jit(solution)/shard_map/ppermute | solution.py:67
  58.1 0.8 scatter_fusion.4
  59.2 3.6 %collective-permute-done.5 = f32[6,2,16,1]{2,1,0,3:T(2,128)S(1)} collective-permute-done((f32[6,2,16,1]{2,1,0,3:T(2,128)S(1)}, f32[6,2,16,1]{2,1,0,3:T(2,128)S(1)}, u32[]{:S(2)}, u32[]{:S(2)}) %collective-permute-start.5) | collective-permute-done | bytes 800 | tf_op jit(solution)/shard_map/ppermute | solution.py:67
  64.8 2.5 %collective-permute-start.7 = (f32[6,1,16,130]{3,2,0,1:T(8,128)S(1)}, f32[6,1,16,130]{3,2,0,1:T(8,128)S(1)}, u32[]{:S(2)}, u32[]{:S(2)}) collective-permute-start(f32[6,1,16,130]{3,2,0,1:T(8,128)S(1)} %bitcast.353), channel_id=1, source_target_pairs={{8,0},{16,8},{24,16},{32,24},{40,32},{48,40},{56,48},{64,56},{72,6... | collective-permute-start | bytes 149768 | tf_op jit(solution)/shard_map/ppermute | solution.py:67
  67.9 2.8 %collective-permute-start.6 = (f32[6,1,16,130]{3,2,0,1:T(8,128)S(1)}, f32[6,1,16,130]{3,2,0,1:T(8,128)S(1)}, u32[]{:S(2)}, u32[]{:S(2)}) collective-permute-start(f32[6,1,16,130]{3,2,0,1:T(8,128)S(1)} %bitcast.351), channel_id=1, source_target_pairs={{760,0},{0,8},{8,16},{16,24},{24,32},{32,40},{40,48},{48,56},{56,6... | collective-permute-start | bytes 149768 | tf_op jit(solution)/shard_map/ppermute | solution.py:67
  70.9 0.7 scatter_fusion.7
  71.7 6.9 %collective-permute-done.6 = f32[6,1,16,130]{3,2,0,1:T(8,128)S(1)} collective-permute-done((f32[6,1,16,130]{3,2,0,1:T(8,128)S(1)}, f32[6,1,16,130]{3,2,0,1:T(8,128)S(1)}, u32[]{:S(2)}, u32[]{:S(2)}) %collective-permute-start.6) | collective-permute-done | bytes 49952 | tf_op jit(solution)/shard_map/ppermute | solution.py:67
  79.7 0.7 slice_bitcast_fusion.20
  81.9 1.0 constant_dynamic-update-slice_fusion.14
  83.9 1.0 copy.152
  85.5 4.4 %collective-permute-start.8 = (f32[5,2,16,1]{2,1,0,3:T(2,128)S(1)}, f32[5,2,16,1]{2,1,0,3:T(2,128)S(1)}, u32[]{:S(2)}, u32[]{:S(2)}) collective-permute-start(f32[5,2,16,1]{2,1,0,3:T(2,128)S(1)} %bitcast.380), channel_id=1, source_target_pairs={{7,0},{0,1},{1,2},{2,3},{3,4},{4,5},{5,6},{6,7},{15,8},{8,9},{9,10... | collective-permute-start | bytes 1928 | tf_op jit(solution)/shard_map/ppermute | solution.py:67
  90.5 1.9 %collective-permute-start.9 = (f32[5,2,16,1]{2,1,0,3:T(2,128)S(1)}, f32[5,2,16,1]{2,1,0,3:T(2,128)S(1)}, u32[]{:S(2)}, u32[]{:S(2)}) collective-permute-start(f32[5,2,16,1]{2,1,0,3:T(2,128)S(1)} %bitcast.378), channel_id=1, source_target_pairs={{1,0},{2,1},{3,2},{4,3},{5,4},{6,5},{7,6},{0,7},{9,8},{10,9},{11,1... | collective-permute-start | bytes 1928 | tf_op jit(solution)/shard_map/ppermute | solution.py:67
  93.4 4.6 %collective-permute-done.9 = f32[5,2,16,1]{2,1,0,3:T(2,128)S(1)} collective-permute-done((f32[5,2,16,1]{2,1,0,3:T(2,128)S(1)}, f32[5,2,16,1]{2,1,0,3:T(2,128)S(1)}, u32[]{:S(2)}, u32[]{:S(2)}) %collective-permute-start.9) | collective-permute-done | bytes 672 | tf_op jit(solution)/shard_map/ppermute | solution.py:67
  99.8 1.9 %collective-permute-start.10 = (f32[5,1,16,130]{3,2,0,1:T(8,128)S(1)}, f32[5,1,16,130]{3,2,0,1:T(8,128)S(1)}, u32[]{:S(2)}, u32[]{:S(2)}) collective-permute-start(f32[5,1,16,130]{3,2,0,1:T(8,128)S(1)} %bitcast.364), channel_id=1, source_target_pairs={{760,0},{0,8},{8,16},{16,24},{24,32},{32,40},{40,48},{48,56},{56,6... | collective-permute-start | bytes 124808 | tf_op jit(solution)/shard_map/ppermute | solution.py:67
  102.3 8.5 %collective-permute-start.11 = (f32[5,1,16,130]{3,2,0,1:T(8,128)S(1)}, f32[5,1,16,130]{3,2,0,1:T(8,128)S(1)}, u32[]{:S(2)}, u32[]{:S(2)}) collective-permute-start(f32[5,1,16,130]{3,2,0,1:T(8,128)S(1)} %bitcast.362), channel_id=1, source_target_pairs={{8,0},{16,8},{24,16},{32,24},{40,32},{48,40},{56,48},{64,56},{72,6... | collective-permute-start | bytes 124808 | tf_op jit(solution)/shard_map/ppermute | solution.py:67
  114.7 0.9 constant_dynamic-update-slice_fusion.33
  116.7 1.3 copy.156
  118.7 5.0 %collective-permute-start.12 = (f32[6,2,16,1]{2,1,0,3:T(2,128)S(1)}, f32[6,2,16,1]{2,1,0,3:T(2,128)S(1)}, u32[]{:S(2)}, u32[]{:S(2)}) collective-permute-start(f32[6,2,16,1]{2,1,0,3:T(2,128)S(1)} %bitcast.376), channel_id=1, source_target_pairs={{7,0},{0,1},{1,2},{2,3},{3,4},{4,5},{5,6},{6,7},{15,8},{8,9},{9,10... | collective-permute-start | bytes 2312 | tf_op jit(solution)/shard_map/ppermute | solution.py:67
  124.3 1.9 %collective-permute-start.13 = (f32[6,2,16,1]{2,1,0,3:T(2,128)S(1)}, f32[6,2,16,1]{2,1,0,3:T(2,128)S(1)}, u32[]{:S(2)}, u32[]{:S(2)}) collective-permute-start(f32[6,2,16,1]{2,1,0,3:T(2,128)S(1)} %bitcast.372), channel_id=1, source_target_pairs={{1,0},{2,1},{3,2},{4,3},{5,4},{6,5},{7,6},{0,7},{9,8},{10,9},{11,1... | collective-permute-start | bytes 2312 | tf_op jit(solution)/shard_map/ppermute | solution.py:67
  127.3 4.6 %collective-permute-done.13 = f32[6,2,16,1]{2,1,0,3:T(2,128)S(1)} collective-permute-done((f32[6,2,16,1]{2,1,0,3:T(2,128)S(1)}, f32[6,2,16,1]{2,1,0,3:T(2,128)S(1)}, u32[]{:S(2)}, u32[]{:S(2)}) %collective-permute-start.13) | collective-permute-done | bytes 800 | tf_op jit(solution)/shard_map/ppermute | solution.py:67
  133.8 1.9 %collective-permute-start.14 = (f32[6,1,16,130]{3,2,0,1:T(8,128)S(1)}, f32[6,1,16,130]{3,2,0,1:T(8,128)S(1)}, u32[]{:S(2)}, u32[]{:S(2)}) collective-permute-start(f32[6,1,16,130]{3,2,0,1:T(8,128)S(1)} %bitcast.352), channel_id=1, source_target_pairs={{760,0},{0,8},{8,16},{16,24},{24,32},{32,40},{40,48},{48,56},{56,6... | collective-permute-start | bytes 149768 | tf_op jit(solution)/shard_map/ppermute | solution.py:67
  136.3 10.9 %collective-permute-start.15 = (f32[6,1,16,130]{3,2,0,1:T(8,128)S(1)}, f32[6,1,16,130]{3,2,0,1:T(8,128)S(1)}, u32[]{:S(2)}, u32[]{:S(2)}) collective-permute-start(f32[6,1,16,130]{3,2,0,1:T(8,128)S(1)} %bitcast.350), channel_id=1, source_target_pairs={{8,0},{16,8},{24,16},{32,24},{40,32},{48,40},{56,48},{64,56},{72,6... | collective-permute-start | bytes 149768 | tf_op jit(solution)/shard_map/ppermute | solution.py:67
  148.7 0.7 scatter_fusion.15
  151.9 0.9 constant_dynamic-update-slice_fusion.49
  (406 shorter events, 35.3 us)
Async XLA Ops:
  0.6 12.1 %copy-start.9 = (s32[5]{0:T(128)S(1)}, s32[5]{0:T(128)}, u32[]{:S(2)}) copy-start(s32[5]{0:T(128)} %constant.422) | copy-start | bytes 64
  0.7 18.1 %copy-start.85 = (s32[5]{0:T(128)S(1)}, s32[5]{0:T(128)}, u32[]{:S(2)}) copy-start(s32[5]{0:T(128)} %constant.411) | copy-start | bytes 64
  0.7 20.4 %copy-start.1 = (f32[15,2,16,128]{3,2,1,0:T(8,128)S(1)}, f32[15,2,16,128]{3,2,1,0:T(8,128)}, u32[]{:S(2)}) copy-start(f32[15,2,16,128]{3,2,1,0:T(8,128)} %param.35) | copy-start | bytes 737284
  3.1 18.2 %copy-start.11 = (s32[5]{0:T(128)S(1)}, s32[5]{0:T(128)}, u32[]{:S(2)}) copy-start(s32[5]{0:T(128)} %constant.439) | copy-start | bytes 64
  3.2 32.1 %copy-start.18 = (s32[5]{0:T(128)S(1)}, s32[5]{0:T(128)}, u32[]{:S(2)}) copy-start(s32[5]{0:T(128)} %constant.438) | copy-start | bytes 64
  3.8 14.9 %collective-permute-start = (f32[5,2,16,1]{2,1,0,3:T(2,128)S(1)}, f32[5,2,16,1]{2,1,0,3:T(2,128)S(1)}, u32[]{:S(2)}, u32[]{:S(2)}) collective-permute-start(f32[5,2,16,1]{2,1,0,3:T(2,128)S(1)} %bitcast.381), channel_id=1, source_target_pairs={{7,0},{0,1},{1,2},{2,3},{3,4},{4,5},{5,6},{6,7},{15,8},{8,9},{9,10... | collective-permute-start | bytes 1928 | tf_op jit(solution)/shard_map/ppermute | solution.py:67
  13.4 6.7 %collective-permute-start.1 = (f32[5,2,16,1]{2,1,0,3:T(2,128)S(1)}, f32[5,2,16,1]{2,1,0,3:T(2,128)S(1)}, u32[]{:S(2)}, u32[]{:S(2)}) collective-permute-start(f32[5,2,16,1]{2,1,0,3:T(2,128)S(1)} %bitcast.379), channel_id=1, source_target_pairs={{1,0},{2,1},{3,2},{4,3},{5,4},{6,5},{7,6},{0,7},{9,8},{10,9},{11,1... | collective-permute-start | bytes 1928 | tf_op jit(solution)/shard_map/ppermute | solution.py:67
  19.7 26.9 %copy-start.82 = (s32[5]{0:T(128)S(1)}, s32[5]{0:T(128)}, u32[]{:S(2)}) copy-start(s32[5]{0:T(128)} %constant.410) | copy-start | bytes 64
  21.9 15.9 %collective-permute-start.3 = (f32[5,1,16,130]{3,2,0,1:T(8,128)S(1)}, f32[5,1,16,130]{3,2,0,1:T(8,128)S(1)}, u32[]{:S(2)}, u32[]{:S(2)}) collective-permute-start(f32[5,1,16,130]{3,2,0,1:T(8,128)S(1)} %bitcast.365), channel_id=1, source_target_pairs={{8,0},{16,8},{24,16},{32,24},{40,32},{48,40},{56,48},{64,56},{72,6... | collective-permute-start | bytes 124808 | tf_op jit(solution)/shard_map/ppermute | solution.py:67
  35.9 10.7 %collective-permute-start.2 = (f32[5,1,16,130]{3,2,0,1:T(8,128)S(1)}, f32[5,1,16,130]{3,2,0,1:T(8,128)S(1)}, u32[]{:S(2)}, u32[]{:S(2)}) collective-permute-start(f32[5,1,16,130]{3,2,0,1:T(8,128)S(1)} %bitcast.363), channel_id=1, source_target_pairs={{760,0},{0,8},{8,16},{16,24},{24,32},{32,40},{40,48},{48,56},{56,6... | collective-permute-start | bytes 124808 | tf_op jit(solution)/shard_map/ppermute | solution.py:67
  49.4 6.1 %copy-start.10 = (s32[6]{0:T(128)S(1)}, s32[6]{0:T(128)}, u32[]{:S(2)}) copy-start(s32[6]{0:T(128)} %constant.458) | copy-start | bytes 76
  50.7 13.5 %copy-start.8 = (s32[6]{0:T(128)S(1)}, s32[6]{0:T(128)}, u32[]{:S(2)}) copy-start(s32[6]{0:T(128)} %constant.475) | copy-start | bytes 76
  51.3 6.7 %collective-permute-start.4 = (f32[6,2,16,1]{2,1,0,3:T(2,128)S(1)}, f32[6,2,16,1]{2,1,0,3:T(2,128)S(1)}, u32[]{:S(2)}, u32[]{:S(2)}) collective-permute-start(f32[6,2,16,1]{2,1,0,3:T(2,128)S(1)} %bitcast.377), channel_id=1, source_target_pairs={{7,0},{0,1},{1,2},{2,3},{3,4},{4,5},{5,6},{6,7},{15,8},{8,9},{9,10... | collective-permute-start | bytes 2312 | tf_op jit(solution)/shard_map/ppermute | solution.py:67
  56.1 6.7 %collective-permute-start.5 = (f32[6,2,16,1]{2,1,0,3:T(2,128)S(1)}, f32[6,2,16,1]{2,1,0,3:T(2,128)S(1)}, u32[]{:S(2)}, u32[]{:S(2)}) collective-permute-start(f32[6,2,16,1]{2,1,0,3:T(2,128)S(1)} %bitcast.373), channel_id=1, source_target_pairs={{1,0},{2,1},{3,2},{4,3},{5,4},{6,5},{7,6},{0,7},{9,8},{10,9},{11,1... | collective-permute-start | bytes 2312 | tf_op jit(solution)/shard_map/ppermute | solution.py:67
  58.1 9.3 %copy-start.14 = (s32[6]{0:T(128)S(1)}, s32[6]{0:T(128)}, u32[]{:S(2)}) copy-start(s32[6]{0:T(128)} %constant.474) | copy-start | bytes 76
  63.9 14.7 %copy-start.80 = (s32[6]{0:T(128)S(1)}, s32[6]{0:T(128)}, u32[]{:S(2)}) copy-start(s32[6]{0:T(128)} %constant.448) | copy-start | bytes 76
  64.8 6.1 %collective-permute-start.7 = (f32[6,1,16,130]{3,2,0,1:T(8,128)S(1)}, f32[6,1,16,130]{3,2,0,1:T(8,128)S(1)}, u32[]{:S(2)}, u32[]{:S(2)}) collective-permute-start(f32[6,1,16,130]{3,2,0,1:T(8,128)S(1)} %bitcast.353), channel_id=1, source_target_pairs={{8,0},{16,8},{24,16},{32,24},{40,32},{48,40},{56,48},{64,56},{72,6... | collective-permute-start | bytes 149768 | tf_op jit(solution)/shard_map/ppermute | solution.py:67
  67.9 10.6 %collective-permute-start.6 = (f32[6,1,16,130]{3,2,0,1:T(8,128)S(1)}, f32[6,1,16,130]{3,2,0,1:T(8,128)S(1)}, u32[]{:S(2)}, u32[]{:S(2)}) collective-permute-start(f32[6,1,16,130]{3,2,0,1:T(8,128)S(1)} %bitcast.351), channel_id=1, source_target_pairs={{760,0},{0,8},{8,16},{16,24},{24,32},{32,40},{40,48},{48,56},{56,6... | collective-permute-start | bytes 149768 | tf_op jit(solution)/shard_map/ppermute | solution.py:67
  80.4 2.9 %copy-start.72 = (f32[2,1,128]{2,1,0:T(1,128)S(1)}, f32[2,1,128]{2,1,0:T(1,128)}, u32[]{:S(2)}) copy-start(f32[2,1,128]{2,1,0:T(1,128)} %copy-done.71) | copy-start | bytes 3076
  80.4 2.9 %copy-start.74 = (f32[2,1,128]{2,1,0:T(1,128)S(1)}, f32[2,1,128]{2,1,0:T(1,128)}, u32[]{:S(2)}) copy-start(f32[2,1,128]{2,1,0:T(1,128)} %copy-done.73) | copy-start | bytes 3076
  83.8 8.7 %copy-start.86 = (s32[5]{0:T(128)S(1)}, s32[5]{0:T(128)}, u32[]{:S(2)}) copy-start(s32[5]{0:T(128)} %constant.411) | copy-start | bytes 64
  84.8 26.0 %copy-start.83 = (s32[5]{0:T(128)S(1)}, s32[5]{0:T(128)}, u32[]{:S(2)}) copy-start(s32[5]{0:T(128)} %constant.410) | copy-start | bytes 64
  85.5 7.0 %collective-permute-start.8 = (f32[5,2,16,1]{2,1,0,3:T(2,128)S(1)}, f32[5,2,16,1]{2,1,0,3:T(2,128)S(1)}, u32[]{:S(2)}, u32[]{:S(2)}) collective-permute-start(f32[5,2,16,1]{2,1,0,3:T(2,128)S(1)} %bitcast.380), channel_id=1, source_target_pairs={{7,0},{0,1},{1,2},{2,3},{3,4},{4,5},{5,6},{6,7},{15,8},{8,9},{9,10... | collective-permute-start | bytes 1928 | tf_op jit(solution)/shard_map/ppermute | solution.py:67
  90.5 7.5 %collective-permute-start.9 = (f32[5,2,16,1]{2,1,0,3:T(2,128)S(1)}, f32[5,2,16,1]{2,1,0,3:T(2,128)S(1)}, u32[]{:S(2)}, u32[]{:S(2)}) collective-permute-start(f32[5,2,16,1]{2,1,0,3:T(2,128)S(1)} %bitcast.378), channel_id=1, source_target_pairs={{1,0},{2,1},{3,2},{4,3},{5,4},{6,5},{7,6},{0,7},{9,8},{10,9},{11,1... | collective-permute-start | bytes 1928 | tf_op jit(solution)/shard_map/ppermute | solution.py:67
  99.8 11.0 %collective-permute-start.10 = (f32[5,1,16,130]{3,2,0,1:T(8,128)S(1)}, f32[5,1,16,130]{3,2,0,1:T(8,128)S(1)}, u32[]{:S(2)}, u32[]{:S(2)}) collective-permute-start(f32[5,1,16,130]{3,2,0,1:T(8,128)S(1)} %bitcast.364), channel_id=1, source_target_pairs={{760,0},{0,8},{8,16},{16,24},{24,32},{32,40},{40,48},{48,56},{56,6... | collective-permute-start | bytes 124808 | tf_op jit(solution)/shard_map/ppermute | solution.py:67
  102.3 10.0 %collective-permute-start.11 = (f32[5,1,16,130]{3,2,0,1:T(8,128)S(1)}, f32[5,1,16,130]{3,2,0,1:T(8,128)S(1)}, u32[]{:S(2)}, u32[]{:S(2)}) collective-permute-start(f32[5,1,16,130]{3,2,0,1:T(8,128)S(1)} %bitcast.362), channel_id=1, source_target_pairs={{8,0},{16,8},{24,16},{32,24},{40,32},{48,40},{56,48},{64,56},{72,6... | collective-permute-start | bytes 124808 | tf_op jit(solution)/shard_map/ppermute | solution.py:67
  116.7 9.5 %copy-start.84 = (s32[6]{0:T(128)S(1)}, s32[6]{0:T(128)}, u32[]{:S(2)}) copy-start(s32[6]{0:T(128)} %constant.449) | copy-start | bytes 76
  118.7 7.6 %collective-permute-start.12 = (f32[6,2,16,1]{2,1,0,3:T(2,128)S(1)}, f32[6,2,16,1]{2,1,0,3:T(2,128)S(1)}, u32[]{:S(2)}, u32[]{:S(2)}) collective-permute-start(f32[6,2,16,1]{2,1,0,3:T(2,128)S(1)} %bitcast.376), channel_id=1, source_target_pairs={{7,0},{0,1},{1,2},{2,3},{3,4},{4,5},{5,6},{6,7},{15,8},{8,9},{9,10... | collective-permute-start | bytes 2312 | tf_op jit(solution)/shard_map/ppermute | solution.py:67
  124.3 7.6 %collective-permute-start.13 = (f32[6,2,16,1]{2,1,0,3:T(2,128)S(1)}, f32[6,2,16,1]{2,1,0,3:T(2,128)S(1)}, u32[]{:S(2)}, u32[]{:S(2)}) collective-permute-start(f32[6,2,16,1]{2,1,0,3:T(2,128)S(1)} %bitcast.372), channel_id=1, source_target_pairs={{1,0},{2,1},{3,2},{4,3},{5,4},{6,5},{7,6},{0,7},{9,8},{10,9},{11,1... | collective-permute-start | bytes 2312 | tf_op jit(solution)/shard_map/ppermute | solution.py:67
  132.6 14.9 %copy-start.81 = (s32[6]{0:T(128)S(1)}, s32[6]{0:T(128)}, u32[]{:S(2)}) copy-start(s32[6]{0:T(128)} %constant.448) | copy-start | bytes 76
  133.8 13.6 %collective-permute-start.14 = (f32[6,1,16,130]{3,2,0,1:T(8,128)S(1)}, f32[6,1,16,130]{3,2,0,1:T(8,128)S(1)}, u32[]{:S(2)}, u32[]{:S(2)}) collective-permute-start(f32[6,1,16,130]{3,2,0,1:T(8,128)S(1)} %bitcast.352), channel_id=1, source_target_pairs={{760,0},{0,8},{8,16},{16,24},{24,32},{32,40},{40,48},{48,56},{56,6... | collective-permute-start | bytes 149768 | tf_op jit(solution)/shard_map/ppermute | solution.py:67
  136.3 12.4 %collective-permute-start.15 = (f32[6,1,16,130]{3,2,0,1:T(8,128)S(1)}, f32[6,1,16,130]{3,2,0,1:T(8,128)S(1)}, u32[]{:S(2)}, u32[]{:S(2)}) collective-permute-start(f32[6,1,16,130]{3,2,0,1:T(8,128)S(1)} %bitcast.350), channel_id=1, source_target_pairs={{8,0},{16,8},{24,16},{32,24},{40,32},{48,40},{56,48},{64,56},{72,6... | collective-permute-start | bytes 149768 | tf_op jit(solution)/shard_map/ppermute | solution.py:67
  (73 other events, 117.4 us)
where the time goes:
time: 156 us; the launch traced here: 155 us
  starting transfers between devices  77.4 us (50%)
  local copies, waits for them, and re-layouts  36.4 us (23%)
  waiting for transfers between devices  29.7 us (19%)
  other arithmetic  8.74 us (6%)
  between operations  2.61 us (2%)
    ppermute x16, starting transfers between devices, shifted(): return lax.ppermute(block, axis, route)  77.4 us
    ppermute x16, waiting for transfers between devices, shifted(): return lax.ppermute(block, axis, route)  29.7 us
    unnamed x64, other arithmetic  6.14 us
    slice x84, local copies, waits for them, and re-layouts, pull_plane(): return jnp.roll(window, vector[2], axis=1)  4.53 us
    scatter x8, local copies, waits for them, and re-layouts, with_rims(): left_column = empty_column.at[jnp.array(upward_rows)].set(upper)  4.08 us
    scatter x8, local copies, waits for them, and re-layouts, with_rims(): right_column = empty_column.at[jnp.array(downward_rows)].set(lower)  3.94 us
    unnamed x179, local copies, waits for them, and re-layouts  3.93 us
  transfers between devices with their start and end apart: 16, of which 10 were waited for; matrix products, arithmetic and copies ran while one was open for 8% of the time, Pallas kernels for 0%

commit v1 on v0

v1 whole, which is shorter than its diff:
```python
import functools

import jax
import jax.numpy as jnp
from jax import lax
from jax.experimental import pallas as pl
from jax.experimental.pallas import tpu as pltpu
from jax.sharding import PartitionSpec as P

HV = [
    (0, 0, 0),
    (1, 0, 0),
    (-1, 0, 0),
    (0, 1, 0),
    (0, -1, 0),
    (0, 0, 1),
    (0, 0, -1),
    (1, 1, 1),
    (1, 1, -1),
    (1, -1, 1),
    (1, -1, -1),
    (-1, 1, 1),
    (-1, 1, -1),
    (-1, -1, 1),
    (-1, -1, -1),
]
HW = [2.0 / 9.0] + [1.0 / 9.0] * 6 + [1.0 / 72.0] * 8
FV = [
    (0, 0, 0),
    (1, 0, 0),
    (-1, 0, 0),
    (0, 1, 0),
    (0, -1, 0),
    (0, 0, 1),
    (0, 0, -1),
    (1, 1, 0),
    (1, -1, 0),
    (-1, 1, 0),
    (-1, -1, 0),
    (1, 0, 1),
    (1, 0, -1),
    (-1, 0, 1),
    (-1, 0, -1),
    (0, 1, 1),
    (0, 1, -1),
    (0, -1, 1),
    (0, -1, -1),
]
FW = [1.0 / 3.0] + [1.0 / 18.0] * 6 + [1.0 / 36.0] * 12
NH, NF = len(HV), len(FV)
BETA = 12.0 * 0.05 / 4.0
KAPPA = 1.5 * 0.05 * 4.0
FLOOR = 0.1
LAMBDA = 0.3
INV_RELAX = 1.0 / 0.8


def neg(v):
    return (-v[0], -v[1], -v[2])


def pairs(velocities):
    return [
        (i, velocities.index(neg(v))) for i, v in enumerate(velocities) if v > neg(v)
    ]


HP, FP = pairs(HV), pairs(FV)
H_FORE = [i for i, v in enumerate(HV) if v[0] == 1]
H_BACK = [i for i, v in enumerate(HV) if v[0] == -1]
F_FORE = [i for i, v in enumerate(FV) if v[0] == 1]
F_BACK = [i for i, v in enumerate(FV) if v[0] == -1]
DEEP = 4
SLOTS = 128 // DEEP
ROWS = [("h", i, r) for i in range(NH) for r in range(2)] + [
    ("f", i, r) for i in range(NF) for r in range(2)
] + [("s", 0, r) for r in range(2)]
EDGE_TILES = -(-len(ROWS) // SLOTS)
SENT = len(H_FORE) + len(F_FORE) + 1
F32 = jnp.float32


def lanes():
    return lax.broadcasted_iota(jnp.int32, (16, 128), 1)


def yroll(tile, shift):
    return pltpu.roll(tile, shift % 128, axis=1)


def zroll(tile, shift):
    return pltpu.roll(tile, shift % 16, axis=0)


def odd(axis):
    return lax.rem(lax.axis_index(axis), 2) == 1


def total(terms):
    terms = list(terms)
    while len(terms) > 1:
        terms = [
            terms[k] + terms[k + 1] if k + 1 < len(terms) else terms[k]
            for k in range(0, len(terms), 2)
        ]
    return terms[0]


class Wide:
    def __init__(self, lane):
        self.first, self.last = lane == 0, lane == 127

    def shift(self, field, c, rim=True):
        if c == 0:
            return field
        edge = self.first if c == 1 else self.last
        own, out = yroll(field[0], c), yroll(field[1], c)
        return (
            jnp.where(edge, out, own),
            jnp.where(edge, own, out) if rim else None,
        )

    def pull(self, field, v, rim=True):
        if v[2]:
            field = (zroll(field[0], v[2]), zroll(field[1], v[2]))
        return self.shift(field, v[1], rim)


def add(a, b):
    return (a[0] + b[0], a[1] + b[1])


def edges_kernel(h_ref, f_ref, s_ref, a_ref, b_ref):
    lane = lanes()
    slot = lane // DEEP
    right = [jnp.zeros((16, 128), F32) for _ in range(EDGE_TILES)]
    left = [jnp.zeros((16, 128), F32) for _ in range(EDGE_TILES)]
    for k, (kind, i, r) in enumerate(ROWS):
        t, s = divmod(k, SLOTS)
        if kind == "s":
            source = (s_ref[r] > 0).astype(F32)
        else:
            source = h_ref[i, r] if kind == "h" else f_ref[i, r]
        turned = yroll(source, DEEP * (s + 1))
        right[t] = jnp.where(slot == s, turned, right[t])
        left[t] = jnp.where(slot == (s + 1) % SLOTS, turned, left[t])
    swap = odd("gy")
    for t in range(EDGE_TILES):
        left_tile = yroll(left[t], -DEEP)
        a_ref[t] = jnp.where(swap, left_tile, right[t])
        b_ref[t] = jnp.where(swap, right[t], left_tile)


def spread_edges(a_ref, b_ref):
    lane = lanes()
    even_slot = lax.rem(lane // DEEP, 2) == 0
    swap = odd("gy")
    mixed = []
    for t in range(EDGE_TILES):
        a, b = a_ref[t], b_ref[t]
        after = jnp.where(swap, b, a)
        before = yroll(jnp.where(swap, a, b), -DEEP)
        mixed.append(
            (jnp.where(even_slot, after, before), jnp.where(even_slot, before, after))
        )
    places = {row: k for k, row in enumerate(ROWS)}

    def rim(kind, i, r):
        t, s = divmod(places[(kind, i, r)], SLOTS)
        return yroll(mixed[t][s % 2], -DEEP * s)

    return rim


def stream(get_h, get_f, hs_ref, fs_ref, sums_ref, a_ref, b_ref, rim_of_f):
    lane = lanes()
    wide = Wide(lane)

    def put(ref, i, r, field):
        for t in range(ref.shape[2]):
            ref[i, r, t] = field[t]

    sent = {"fore": [], "back": []}
    part = {"fore": [], "back": []}
    for i, v in enumerate(HV):
        pulled = [wide.pull(get_h(i, r), v) for r in range(2)]
        if v[0] == 0:
            put(hs_ref, i, 0, pulled[0])
            put(hs_ref, i, 1, pulled[1])
            part["fore"].append(pulled[1])
            part["back"].append(pulled[0])
        elif v[0] == 1:
            put(hs_ref, i, 1, pulled[0])
            sent["fore"].append(pulled[1])
            part["fore"].append(pulled[0])
        else:
            put(hs_ref, i, 0, pulled[1])
            sent["back"].append(pulled[0])
            part["back"].append(pulled[1])
    for n, way in enumerate(("fore", "back")):
        kept = functools.reduce(add, sent[way])
        sums_ref[n, 0] = kept[0]
        sums_ref[n, 1] = kept[1]
    for i, v in enumerate(FV):
        pulled = [wide.pull(get_f(i, r), v, rim_of_f) for r in range(2)]
        if v[0] == 0:
            put(fs_ref, i, 0, pulled[0])
            put(fs_ref, i, 1, pulled[1])
        elif v[0] == 1:
            put(fs_ref, i, 1, pulled[0])
            sent["fore"].append(pulled[1])
        else:
            put(fs_ref, i, 0, pulled[1])
            sent["back"].append(pulled[0])
    swap = odd("gx")
    packed = []
    for way in ("fore", "back"):
        fields = sent[way] + [functools.reduce(add, part[way])]
        rims = jnp.zeros((16, 128), F32)
        for j, field in enumerate(fields):
            if field[1] is not None:
                rims = jnp.where(lane // 8 == j, yroll(field[1], 8 * j + 4), rims)
        packed.append([field[0] for field in fields] + [rims])
    for j in range(SENT + 1):
        a_ref[j] = jnp.where(swap, packed[1][j], packed[0][j])
        b_ref[j] = jnp.where(swap, packed[0][j], packed[1][j])


def collide(hs_ref, fs_ref, sums_ref, a_ref, b_ref, solid_of, new_h, new_f, scratch, tiles):
    got_ref, phi_ref, grad_ref = scratch
    lane = lanes()
    wide = Wide(lane)
    swap = odd("gx")
    rims = (
        jnp.where(swap, a_ref[SENT], b_ref[SENT]),
        jnp.where(swap, b_ref[SENT], a_ref[SENT]),
    )
    for j in range(SENT):
        a, b = a_ref[j], b_ref[j]
        got_ref[0, j, 0] = jnp.where(swap, a, b)
        got_ref[1, j, 0] = jnp.where(swap, b, a)
        for n in range(2):
            got_ref[n, j, 1] = yroll(rims[n], -(8 * j + 4))

    def h_at(i, r, t, zs):
        if r == 0 and HV[i][0] == 1:
            return got_ref[0, H_FORE.index(i), t, zs]
        if r == 1 and HV[i][0] == -1:
            return got_ref[1, H_BACK.index(i), t, zs]
        return hs_ref[i, r, t, zs]

    def f_at(i, r, t, zs):
        if r == 0 and FV[i][0] == 1:
            return got_ref[0, len(H_FORE) + F_FORE.index(i), t, zs]
        if r == 1 and FV[i][0] == -1:
            return got_ref[1, len(H_BACK) + F_BACK.index(i), t, zs]
        return fs_ref[i, r, t, zs]

    every = slice(None)
    for t in range(2):
        phi_ref[0, t] = got_ref[0, SENT - 1, t] + sums_ref[1, t]
        phi_ref[3, t] = got_ref[1, SENT - 1, t] + sums_ref[0, t]
        for r in range(2):
            phi_ref[r + 1, t] = total(h_at(i, r, t, every) for i in range(NH))
    for r in range(2):
        below, own, above = [(phi_ref[q, 0], phi_ref[q, 1]) for q in (r, r + 1, r + 2)]
        across = (above[0] - below[0], above[1] - below[1])
        around = add(above, below)
        upright = tuple(zroll(own[t], 1) + zroll(own[t], -1) for t in range(2))
        third = tuple(
            (1.0 / 3.0) * own[t] + (1.0 / 6.0) * (around[t] + upright[t]) for t in range(2)
        )
        rim = tiles == 2
        third_up, third_down = wide.shift(third, -1, rim), wide.shift(third, 1, rim)
        across_up, across_down = wide.shift(across, -1, rim), wide.shift(across, 1, rim)
        own_up, own_down = wide.shift(own, -1, rim), wide.shift(own, 1, rim)
        for t in range(tiles):
            along_y = own_up[t] + own_down[t]
            level = (1.0 / 6.0) * own[t] + (1.0 / 12.0) * (around[t] + along_y)
            grad_ref[r, t, 0] = (1.0 / 6.0) * across[t] + (1.0 / 12.0) * (
                across_up[t] + across_down[t] + zroll(across[t], 1) + zroll(across[t], -1)
            )
            grad_ref[r, t, 1] = 0.5 * (third_up[t] - third_down[t])
            grad_ref[r, t, 2] = zroll(level, -1) - zroll(level, 1)
            grad_ref[r, t, 3] = (
                (1.0 / 3.0) * (around[t] + upright[t])
                + (1.0 / 6.0) * (zroll(around[t], 1) + zroll(around[t], -1))
                + (third_up[t] + third_down[t])
                - 4.0 * own[t]
            )
    for r in range(2):
        for t in range(tiles):
            for z in (0, 8):
                zs = slice(z, z + 8)
                solid = solid_of(r, t, zs)
                phi = phi_ref[r + 1, t, zs]
                grad = [grad_ref[r, t, n, zs] for n in range(3)]
                collide_part(
                    phi,
                    grad,
                    grad_ref[r, t, 3, zs],
                    solid,
                    lambda i, r=r, t=t, zs=zs: h_at(i, r, t, zs),
                    lambda i, r=r, t=t, zs=zs: f_at(i, r, t, zs),
                    functools.partial(new_h, r, t, zs),
                    functools.partial(new_f, r, t, zs),
                )


def dot(v, u):
    terms = [(s, c) for s, c in zip(v, u, strict=True) if s]
    out = None
    for s, c in terms:
        if out is None:
            out = c if s > 0 else -c
        else:
            out = out + c if s > 0 else out - c
    return out


def collide_part(phi, grad, laplacian, solid, h_at, f_at, put_h, put_f):
    clipped = jnp.clip(phi, 0.0, 1.0)
    density = 1.0 + 2.0 * clipped
    relax = 0.6 + 0.4 * clipped
    inverse = 1.0 / (density * relax)
    rate, per_density = density * inverse, relax * inverse
    potential = (4.0 * BETA) * phi * (phi - 1.0) * (phi - 0.5) - KAPPA * laplacian
    force = [potential * g for g in grad]
    squared = grad[0] * grad[0] + grad[1] * grad[1] + grad[2] * grad[2]
    scale = 1.0 / jnp.maximum(jnp.sqrt(squared), FLOOR)
    f_rest = f_at(0)
    moment = [0.5 * c for c in force]
    pressure = f_rest
    for i, o in FP:
        fi, fo = f_at(i), f_at(o)
        difference = fi - fo
        pressure = pressure + (fi + fo)
        for n in range(3):
            if FV[i][n]:
                moment[n] = (
                    moment[n] + difference if FV[i][n] > 0 else moment[n] - difference
                )
    u = [m * per_density for m in moment]
    speed = u[0] * u[0] + u[1] * u[1] + u[2] * u[2]
    pull = 3.0 * (1.0 - 0.5 * rate) * per_density
    drive = [3.0 * rate * u[n] + pull * force[n] for n in range(3)]
    keep = 1.0 - rate
    level = rate * (pressure - 1.5 * speed)
    bend = 4.5 * rate
    put_f(0, jnp.where(solid, f_rest, keep * f_rest + FW[0] * level))
    for i, o in FP:
        w = FW[i]
        fi, fo = f_at(i), f_at(o)
        along = dot(FV[i], u)
        even = w * (level + bend * (along * along))
        uneven = w * dot(FV[i], drive)
        put_f(i, jnp.where(solid, fo, keep * fi + (even + uneven)))
        put_f(o, jnp.where(solid, fi, keep * fo + (even - uneven)))
    sharp = LAMBDA * phi * (1.0 - phi) * scale
    drift = [3.0 * phi * u[n] + sharp * grad[n] for n in range(3)]
    h_rest = h_at(0)
    stay = 1.0 - INV_RELAX
    put_h(0, jnp.where(solid, h_rest, stay * h_rest + (INV_RELAX * HW[0]) * phi))
    for i, o in HP:
        w = INV_RELAX * HW[i]
        hi, ho = h_at(i), h_at(o)
        even = w * phi
        uneven = w * dot(HV[i], drift)
        put_h(i, jnp.where(solid, ho, stay * hi + (even + uneven)))
        put_h(o, jnp.where(solid, hi, stay * ho + (even - uneven)))


def first_kernel(h_ref, f_ref, s_ref, ya_ref, yb_ref, a_ref, b_ref, hs_ref, fs_ref, sums_ref, so_ref):
    rim = spread_edges(ya_ref, yb_ref)
    for r in range(2):
        so_ref[r, 0] = (s_ref[r] > 0).astype(F32)
        so_ref[r, 1] = rim("s", 0, r)
    stream(
        lambda i, r: (h_ref[i, r], rim("h", i, r)),
        lambda i, r: (f_ref[i, r], rim("f", i, r)),
        hs_ref,
        fs_ref,
        sums_ref,
        a_ref,
        b_ref,
        True,
    )


def middle_kernel(
    hs_ref, fs_ref, sums_ref, s_ref, ra_ref, rb_ref,
    a_ref, b_ref, hs2_ref, fs2_ref, sums2_ref,
    h1_ref, f1_ref, got_ref, phi_ref, grad_ref,
):
    def new_h(r, t, zs, i, value):
        h1_ref[i, r, t, zs] = value

    def new_f(r, t, zs, i, value):
        f1_ref[i, r, t, zs] = value

    collide(
        hs_ref,
        fs_ref,
        sums_ref,
        ra_ref,
        rb_ref,
        lambda r, t, zs: s_ref[r, t, zs] > 0.5,
        new_h,
        new_f,
        (got_ref, phi_ref, grad_ref),
        2,
    )
    stream(
        lambda i, r: (h1_ref[i, r, 0], h1_ref[i, r, 1]),
        lambda i, r: (f1_ref[i, r, 0], f1_ref[i, r, 1]),
        hs2_ref,
        fs2_ref,
        sums2_ref,
        a_ref,
        b_ref,
        False,
    )


def last_kernel(
    hs_ref, fs_ref, sums_ref, s_ref, ra_ref, rb_ref,
    h_ref, f_ref,
    got_ref, phi_ref, grad_ref,
):
    def new_h(r, t, zs, i, value):
        h_ref[i, r, zs] = value

    def new_f(r, t, zs, i, value):
        f_ref[i, r, zs] = value

    collide(
        hs_ref,
        fs_ref,
        sums_ref,
        ra_ref,
        rb_ref,
        lambda r, t, zs: s_ref[r, t, zs] > 0.5,
        new_h,
        new_f,
        (got_ref, phi_ref, grad_ref),
        1,
    )


def call(kernel, outs, *args, scratch=()):
    spec = pl.BlockSpec(memory_space=pltpu.VMEM)
    return pl.pallas_call(
        kernel,
        out_shape=[jax.ShapeDtypeStruct(shape, F32) for shape in outs],
        in_specs=[spec] * len(args),
        out_specs=[spec] * len(outs),
        scratch_shapes=[pltpu.VMEM(shape, F32) for shape in scratch],
        compiler_params=pltpu.CompilerParams(vmem_limit_bytes=LIMIT),
    )(*args)


def swap_near(block, axis):
    return lax.ppermute(block, axis, [(i, i ^ 1) for i in range(lax.axis_size(axis))])


def swap_far(block, axis):
    n = lax.axis_size(axis)
    route = [(i, (i + 1) % n if i % 2 else (i - 1) % n) for i in range(n)]
    return lax.ppermute(block, axis, route)


TILE = (16, 128)
LIMIT = 16 * 1024 * 1024


def shards(phase_pops, flow_pops, solid_flags):
    edge, sent = (EDGE_TILES, *TILE), (SENT + 1, *TILE)
    a, b = call(edges_kernel, [edge, edge], phase_pops, flow_pops, solid_flags)
    a, b = swap_near(a, "gy"), swap_far(b, "gy")
    wide_h, wide_f = (NH, 2, 2, *TILE), (NF, 2, 2, *TILE)
    sums = (2, 2, *TILE)
    scratch = [(2, SENT, 2, *TILE), (4, 2, *TILE), (2, 2, 4, *TILE)]
    a, b, hs, fs, kept, solid = call(
        first_kernel,
        [sent, sent, wide_h, wide_f, sums, (2, 2, *TILE)],
        phase_pops,
        flow_pops,
        solid_flags,
        a,
        b,
    )
    a, b = swap_near(a, "gx"), swap_far(b, "gx")
    a, b, hs, fs, kept = call(
        middle_kernel,
        [sent, sent, wide_h, (NF, 2, 1, *TILE), sums],
        hs,
        fs,
        kept,
        solid,
        a,
        b,
        scratch=[wide_h, wide_f, *scratch],
    )
    a, b = swap_near(a, "gx"), swap_far(b, "gx")
    return tuple(
        call(
            last_kernel,
            [(NH, 2, *TILE), (NF, 2, *TILE)],
            hs,
            fs,
            kept,
            solid,
            a,
            b,
            scratch=scratch,
        )
    )


def solution(mesh):
    placed = (P(None, "gx", None, "gy"), P(None, "gx", None, "gy"), P("gx", None, "gy"))
    return jax.shard_map(
        shards,
        mesh=mesh,
        in_specs=placed,
        out_specs=placed[:2],
        check_vma=False,
    )
```

time: 156 us -> 54.3 us (0.35)
  the two profiles are of different devices: /device:TPU:1 before, /device:TPU:32 now
where the time goes in v1:
time: 54.3 us; the launch traced here: 53.9 us
  starting transfers between devices  33 us (61%)
  waiting for transfers between devices  13.9 us (26%)
  Pallas kernels  3.68 us (7%)
  local copies, waits for them, and re-layouts  2.62 us (5%)
  between operations  0.72 us (1%)
    ppermute x3, starting transfers between devices, swap_far(): return lax.ppermute(block, axis, route)  25.6 us
    ppermute x3, waiting for transfers between devices, swap_far(): return lax.ppermute(block, axis, route)  13.9 us
    ppermute x3, starting transfers between devices, swap_near(): lax.ppermute(block, axis, [(i, i ^ 1) for i in range(lax.axis_size(axis))])  7.47 us
    pallas_call x4, Pallas kernels, call(): pl.pallas_call(kernel, out_shape=[jax.ShapeDtypeStruct(shape, F32) for sh...  3.68 us
    unnamed x6, local copies, waits for them, and re-layouts  2.62 us
  transfers between devices with their start and end apart: 6, of which 3 were waited for; matrix products, arithmetic and copies ran while one was open for 0% of the time, Pallas kernels for 0%

profile of v1, /device:TPU:32, one launch (start us, length us, event | category | flops | bytes accessed | tf_op | source)
XLA Modules:
  0.0 53.9 jit_solution(4845533573300851723)
XLA Ops:
  0.6 0.0 copy-start
  0.6 1.0 %copy-done = f32[19,2,16,128]{3,2,1,0:T(8,128)S(1)} copy-done((f32[19,2,16,128]{3,2,1,0:T(8,128)S(1)}, f32[19,2,16,128]{3,2,1,0:T(8,128)}, u32[]{:S(2)}) %copy-start) | copy-done | bytes 311320
  1.6 0.0 copy-start.1
  1.6 0.9 %copy-done.1 = f32[15,2,16,128]{3,2,1,0:T(8,128)S(1)} copy-done((f32[15,2,16,128]{3,2,1,0:T(8,128)S(1)}, f32[15,2,16,128]{3,2,1,0:T(8,128)}, u32[]{:S(2)}) %copy-start.1) | copy-done | bytes 245784
  2.5 0.0 copy-start.2
  2.5 0.7 %copy-done.2 = s32[2,16,128]{2,1,0:T(8,128)S(1)} copy-done((s32[2,16,128]{2,1,0:T(8,128)S(1)}, s32[2,16,128]{2,1,0:T(8,128)}, u32[]{:S(2)}) %copy-start.2) | copy-done | bytes 16408
  3.3 0.3 shard_map.50
  3.5 1.9 %collective-permute-start = (f32[3,16,128]{2,1,0:T(8,128)S(1)}, f32[3,16,128]{2,1,0:T(8,128)S(1)}, u32[]{:S(2)}, u32[]{:S(2)}) collective-permute-start(f32[3,16,128]{2,1,0:T(8,128)S(1)} %get-tuple-element.15), channel_id=1, source_target_pairs={{0,1},{1,0},{2,3},{3,2},{4,5},{5,4},{6,7},{7,6},{8,9},{9,8},{10,11... | collective-permute-start | bytes 73736 | tf_op jit(solution)/shard_map/ppermute | solution.py:463
  5.5 14.7 %collective-permute-start.1 = (f32[3,16,128]{2,1,0:T(8,128)S(1)}, f32[3,16,128]{2,1,0:T(8,128)S(1)}, u32[]{:S(2)}, u32[]{:S(2)}) collective-permute-start(f32[3,16,128]{2,1,0:T(8,128)S(1)} %get-tuple-element.16), channel_id=1, source_target_pairs={{0,7},{1,2},{2,1},{3,4},{4,3},{5,6},{6,5},{7,0},{8,15},{9,10},{10,... | collective-permute-start | bytes 73736 | tf_op jit(solution)/shard_map/ppermute | solution.py:469
  20.1 0.0 collective-permute-done.ya_ref
  20.1 1.5 %collective-permute-done.1.yb_ref = f32[3,16,128]{2,1,0:T(8,128)S(1)} collective-permute-done((f32[3,16,128]{2,1,0:T(8,128)S(1)}, f32[3,16,128]{2,1,0:T(8,128)S(1)}, u32[]{:S(2)}, u32[]{:S(2)}) %collective-permute-start.1) | collective-permute-done | bytes 24608 | tf_op jit(solution)/shard_map/ppermute | solution.py:469
  21.7 1.6 %shard_map.51 = (f32[12,16,128]{2,1,0:T(8,128)S(1)}, f32[12,16,128]{2,1,0:T(8,128)S(1)}, f32[15,2,2,16,128]{4,3,2,1,0:T(8,128)S(1)}, f32[19,2,2,16,128]{4,3,2,1,...) custom-call(f32[15,2,16,128]{3,2,1,0:T(8,128)S(1)} %copy-done.1, ...), custom_call_target="tpu_custom_call" | custom-call | tf_op jit(solution)/shard_map/pallas_call | solution.py:452
  23.3 3.6 %collective-permute-start.2 = (f32[12,16,128]{2,1,0:T(8,128)S(1)}, f32[12,16,128]{2,1,0:T(8,128)S(1)}, u32[]{:S(2)}, u32[]{:S(2)}) collective-permute-start(f32[12,16,128]{2,1,0:T(8,128)S(1)} %get-tuple-element.21), channel_id=1, source_target_pairs={{0,8},{8,0},{16,24},{24,16},{32,40},{40,32},{48,56},{56,48},{64,72... | collective-permute-start | bytes 294920 | tf_op jit(solution)/shard_map/ppermute | solution.py:463
  26.9 5.5 %collective-permute-start.3 = (f32[12,16,128]{2,1,0:T(8,128)S(1)}, f32[12,16,128]{2,1,0:T(8,128)S(1)}, u32[]{:S(2)}, u32[]{:S(2)}) collective-permute-start(f32[12,16,128]{2,1,0:T(8,128)S(1)} %get-tuple-element.22), channel_id=1, source_target_pairs={{0,760},{8,16},{16,8},{24,32},{32,24},{40,48},{48,40},{56,64},{64,... | collective-permute-start | bytes 294920 | tf_op jit(solution)/shard_map/ppermute | solution.py:469
  32.4 0.0 collective-permute-done.2.ra_ref
  32.4 6.2 %collective-permute-done.3.rb_ref = f32[12,16,128]{2,1,0:T(8,128)S(1)} collective-permute-done((f32[12,16,128]{2,1,0:T(8,128)S(1)}, f32[12,16,128]{2,1,0:T(8,128)S(1)}, u32[]{:S(2)}, u32[]{:S(2)}) %collective-permute-start.3) | collective-permute-done | bytes 98336 | tf_op jit(solution)/shard_map/ppermute | solution.py:469
  38.5 0.7 %shard_map.52 = (f32[12,16,128]{2,1,0:T(8,128)S(1)}, f32[12,16,128]{2,1,0:T(8,128)S(1)}, f32[15,2,2,16,128]{4,3,2,1,0:T(8,128)S(1)}, f32[19,2,1,16,128]{4,3,2,1,0:T(8,128)S(1)}, f32[2,2,16,128]{3,2,1,0:T(8,128)S(1)}) custom-call(f32[15,2,2,16,128]{4,3,2,1,0:T(8,128)S(1)} %get-tuple-element.17.hs_ref, f32[19,2,2,16,128]{4,3,2,1,0:T(8,128)S(1)} %get-tuple-element.18.fs_ref, ...), custom_call_target="tpu_custom_call" | custom-call | tf_op jit(solution)/shard_map/pallas_call | solution.py:452
  39.2 1.9 %collective-permute-start.4 = (f32[12,16,128]{2,1,0:T(8,128)S(1)}, f32[12,16,128]{2,1,0:T(8,128)S(1)}, u32[]{:S(2)}, u32[]{:S(2)}) collective-permute-start(f32[12,16,128]{2,1,0:T(8,128)S(1)} %get-tuple-element.26), channel_id=1, source_target_pairs={{0,8},{8,0},{16,24},{24,16},{32,40},{40,32},{48,56},{56,48},{64,72... | collective-permute-start | bytes 294920 | tf_op jit(solution)/shard_map/ppermute | solution.py:463
  41.2 5.5 %collective-permute-start.5 = (f32[12,16,128]{2,1,0:T(8,128)S(1)}, f32[12,16,128]{2,1,0:T(8,128)S(1)}, u32[]{:S(2)}, u32[]{:S(2)}) collective-permute-start(f32[12,16,128]{2,1,0:T(8,128)S(1)} %get-tuple-element.27), channel_id=1, source_target_pairs={{0,760},{8,16},{16,8},{24,32},{32,24},{40,48},{48,40},{56,64},{64,... | collective-permute-start | bytes 294920 | tf_op jit(solution)/shard_map/ppermute | solution.py:469
  46.6 0.0 collective-permute-done.4.ra_ref
  46.6 6.2 %collective-permute-done.5.rb_ref = f32[12,16,128]{2,1,0:T(8,128)S(1)} collective-permute-done((f32[12,16,128]{2,1,0:T(8,128)S(1)}, f32[12,16,128]{2,1,0:T(8,128)S(1)}, u32[]{:S(2)}, u32[]{:S(2)}) %collective-permute-start.5) | collective-permute-done | bytes 98336 | tf_op jit(solution)/shard_map/ppermute | solution.py:469
  52.8 1.1 %shard_map.53 = (f32[15,2,16,128]{3,2,1,0:T(8,128)}, f32[19,2,16,128]{3,2,1,0:T(8,128)}) custom-call(f32[15,2,2,16,128]{4,3,2,1,0:T(8,128)S(1)} %get-tuple-element.23.hs_ref, f32[19,2,1,16,128]{4,3,2,1,0:T(8,128)S(1)} %get-tuple-element.24.fs_ref, f32[2,2,16,128]{3,2,1,0:T(8,128)S(1)} %get-tuple-element.25.sums_ref, ...), custom_call_target="tpu_custom_call" | custom-call | tf_op jit(solution)/shard_map/pallas_call | solution.py:452
Async XLA Ops:
  0.6 1.0 %copy-start = (f32[19,2,16,128]{3,2,1,0:T(8,128)S(1)}, f32[19,2,16,128]{3,2,1,0:T(8,128)}, u32[]{:S(2)}) copy-start(f32[19,2,16,128]{3,2,1,0:T(8,128)} %f_ref.3) | copy-start | bytes 933892
  1.6 0.9 %copy-start.1 = (f32[15,2,16,128]{3,2,1,0:T(8,128)S(1)}, f32[15,2,16,128]{3,2,1,0:T(8,128)}, u32[]{:S(2)}) copy-start(f32[15,2,16,128]{3,2,1,0:T(8,128)} %h_ref.3) | copy-start | bytes 737284
  2.5 0.7 %copy-start.2 = (s32[2,16,128]{2,1,0:T(8,128)S(1)}, s32[2,16,128]{2,1,0:T(8,128)}, u32[]{:S(2)}) copy-start(s32[2,16,128]{2,1,0:T(8,128)} %s_ref.3) | copy-start | bytes 49156
  3.5 16.6 %collective-permute-start = (f32[3,16,128]{2,1,0:T(8,128)S(1)}, f32[3,16,128]{2,1,0:T(8,128)S(1)}, u32[]{:S(2)}, u32[]{:S(2)}) collective-permute-start(f32[3,16,128]{2,1,0:T(8,128)S(1)} %get-tuple-element.15), channel_id=1, source_target_pairs={{0,1},{1,0},{2,3},{3,2},{4,5},{5,4},{6,7},{7,6},{8,9},{9,8},{10,11... | collective-permute-start | bytes 73736 | tf_op jit(solution)/shard_map/ppermute | solution.py:463
  5.5 16.2 %collective-permute-start.1 = (f32[3,16,128]{2,1,0:T(8,128)S(1)}, f32[3,16,128]{2,1,0:T(8,128)S(1)}, u32[]{:S(2)}, u32[]{:S(2)}) collective-permute-start(f32[3,16,128]{2,1,0:T(8,128)S(1)} %get-tuple-element.16), channel_id=1, source_target_pairs={{0,7},{1,2},{2,1},{3,4},{4,3},{5,6},{6,5},{7,0},{8,15},{9,10},{10,... | collective-permute-start | bytes 73736 | tf_op jit(solution)/shard_map/ppermute | solution.py:469
  23.3 9.1 %collective-permute-start.2 = (f32[12,16,128]{2,1,0:T(8,128)S(1)}, f32[12,16,128]{2,1,0:T(8,128)S(1)}, u32[]{:S(2)}, u32[]{:S(2)}) collective-permute-start(f32[12,16,128]{2,1,0:T(8,128)S(1)} %get-tuple-element.21), channel_id=1, source_target_pairs={{0,8},{8,0},{16,24},{24,16},{32,40},{40,32},{48,56},{56,48},{64,72... | collective-permute-start | bytes 294920 | tf_op jit(solution)/shard_map/ppermute | solution.py:463
  26.9 11.6 %collective-permute-start.3 = (f32[12,16,128]{2,1,0:T(8,128)S(1)}, f32[12,16,128]{2,1,0:T(8,128)S(1)}, u32[]{:S(2)}, u32[]{:S(2)}) collective-permute-start(f32[12,16,128]{2,1,0:T(8,128)S(1)} %get-tuple-element.22), channel_id=1, source_target_pairs={{0,760},{8,16},{16,8},{24,32},{32,24},{40,48},{48,40},{56,64},{64,... | collective-permute-start | bytes 294920 | tf_op jit(solution)/shard_map/ppermute | solution.py:469
  39.2 7.4 %collective-permute-start.4 = (f32[12,16,128]{2,1,0:T(8,128)S(1)}, f32[12,16,128]{2,1,0:T(8,128)S(1)}, u32[]{:S(2)}, u32[]{:S(2)}) collective-permute-start(f32[12,16,128]{2,1,0:T(8,128)S(1)} %get-tuple-element.26), channel_id=1, source_target_pairs={{0,8},{8,0},{16,24},{24,16},{32,40},{40,32},{48,56},{56,48},{64,72... | collective-permute-start | bytes 294920 | tf_op jit(solution)/shard_map/ppermute | solution.py:463
  41.2 11.6 %collective-permute-start.5 = (f32[12,16,128]{2,1,0:T(8,128)S(1)}, f32[12,16,128]{2,1,0:T(8,128)S(1)}, u32[]{:S(2)}, u32[]{:S(2)}) collective-permute-start(f32[12,16,128]{2,1,0:T(8,128)S(1)} %get-tuple-element.27), channel_id=1, source_target_pairs={{0,760},{8,16},{16,8},{24,32},{32,24},{40,48},{48,40},{56,64},{64,... | collective-permute-start | bytes 294920 | tf_op jit(solution)/shard_map/ppermute | solution.py:469

commit v2 on v1

--- a/solution.py
+++ b/solution.py
@@ -96,6 +96,13 @@
     return lax.rem(lax.axis_index(axis), 2) == 1
 
 
+def partner(ref, j, swap, near):
+    if len(ref.shape) == 3:
+        return ref[j]
+    first, second = ref[0, j], ref[1, j]
+    return jnp.where(swap, first, second) if near else jnp.where(swap, second, first)
+
+
 def total(terms):
     terms = list(terms)
     while len(terms) > 1:
@@ -104,6 +111,11 @@
             for k in range(0, len(terms), 2)
         ]
     return terms[0]
+
+
+def put(ref, i, r, field):
+    for t in range(ref.shape[2]):
+        ref[i, r, t] = field[t]
 
 
 class Wide:
@@ -130,9 +142,12 @@
     return (a[0] + b[0], a[1] + b[1])
 
 
-def edges_kernel(h_ref, f_ref, s_ref, a_ref, b_ref):
-    lane = lanes()
-    slot = lane // DEEP
+def slots_kernel(slot_ref):
+    slot_ref[...] = lanes() // DEEP
+
+
+def edges_kernel(slot_ref, h_ref, f_ref, s_ref, a_ref, b_ref):
+    slot = slot_ref[...]
     right = [jnp.zeros((16, 128), F32) for _ in range(EDGE_TILES)]
     left = [jnp.zeros((16, 128), F32) for _ in range(EDGE_TILES)]
     for k, (kind, i, r) in enumerate(ROWS):
@@ -157,7 +172,7 @@
     swap = odd("gy")
     mixed = []
     for t in range(EDGE_TILES):
-        a, b = a_ref[t], b_ref[t]
+        a, b = partner(a_ref, t, swap, True), partner(b_ref, t, swap, False)
         after = jnp.where(swap, b, a)
         before = yroll(jnp.where(swap, a, b), -DEEP)
         mixed.append(
@@ -172,14 +187,9 @@
     return rim
 
 
-def stream(get_h, get_f, hs_ref, fs_ref, sums_ref, a_ref, b_ref, rim_of_f):
+def stream(get_h, get_f, hs_ref, sums_ref, a_ref, b_ref, rim_of_f):
     lane = lanes()
     wide = Wide(lane)
-
-    def put(ref, i, r, field):
-        for t in range(ref.shape[2]):
-            ref[i, r, t] = field[t]
-
     sent = {"fore": [], "back": []}
     part = {"fore": [], "back": []}
     for i, v in enumerate(HV):
@@ -201,17 +211,10 @@
         kept = functools.reduce(add, sent[way])
         sums_ref[n, 0] = kept[0]
         sums_ref[n, 1] = kept[1]
-    for i, v in enumerate(FV):
-        pulled = [wide.pull(get_f(i, r), v, rim_of_f) for r in range(2)]
-        if v[0] == 0:
-            put(fs_ref, i, 0, pulled[0])
-            put(fs_ref, i, 1, pulled[1])
-        elif v[0] == 1:
-            put(fs_ref, i, 1, pulled[0])
-            sent["fore"].append(pulled[1])
-        else:
-            put(fs_ref, i, 0, pulled[1])
-            sent["back"].append(pulled[0])
+    for i in F_FORE:
+        sent["fore"].append(wide.pull(get_f(i, 1), FV[i], rim_of_f))
+    for i in F_BACK:
+        sent["back"].append(wide.pull(get_f(i, 0), FV[i], rim_of_f))
     swap = odd("gx")
     packed = []
     for way in ("fore", "back"):
@@ -226,17 +229,23 @@
         b_ref[j] = jnp.where(swap, packed[0][j], packed[1][j])
 
 
-def collide(hs_ref, fs_ref, sums_ref, a_ref, b_ref, solid_of, new_h, new_f, scratch, tiles):
+def stream_rest(get_f, fs_ref):
+    wide = Wide(lanes())
+    for i, v in enumerate(FV):
+        for r in range(2):
+            if 0 <= r + v[0] < 2:
+                put(fs_ref, i, r + v[0], wide.pull(get_f(i, r), v, fs_ref.shape[2] == 2))
+
+
+def collide(hs_ref, fs_ref, sums_ref, a_ref, b_ref, solid_of, new_h, new_f, scratch, tiles, row_done=None):
     got_ref, phi_ref, grad_ref = scratch
     lane = lanes()
     wide = Wide(lane)
     swap = odd("gx")
-    rims = (
-        jnp.where(swap, a_ref[SENT], b_ref[SENT]),
-        jnp.where(swap, b_ref[SENT], a_ref[SENT]),
-    )
+    a, b = partner(a_ref, SENT, swap, True), partner(b_ref, SENT, swap, False)
+    rims = jnp.where(swap, a, b), jnp.where(swap, b, a)
     for j in range(SENT):
-        a, b = a_ref[j], b_ref[j]
+        a, b = partner(a_ref, j, swap, True), partner(b_ref, j, swap, False)
         got_ref[0, j, 0] = jnp.where(swap, a, b)
         got_ref[1, j, 0] = jnp.where(swap, b, a)
         for n in range(2):
@@ -305,6 +314,8 @@
                     functools.partial(new_h, r, t, zs),
                     functools.partial(new_f, r, t, zs),
                 )
+        if row_done is not None:
+            row_done(r)
 
 
 def dot(v, u):
@@ -370,7 +381,7 @@
         put_h(o, jnp.where(solid, hi, stay * ho + (even - uneven)))
 
 
-def first_kernel(h_ref, f_ref, s_ref, ya_ref, yb_ref, a_ref, b_ref, hs_ref, fs_ref, sums_ref, so_ref):
+def first_kernel(h_ref, f_ref, s_ref, ya_ref, yb_ref, a_ref, b_ref, hs_ref, sums_ref, so_ref):
     rim = spread_edges(ya_ref, yb_ref)
     for r in range(2):
         so_ref[r, 0] = (s_ref[r] > 0).astype(F32)
@@ -379,7 +390,6 @@
         lambda i, r: (h_ref[i, r], rim("h", i, r)),
         lambda i, r: (f_ref[i, r], rim("f", i, r)),
         hs_ref,
-        fs_ref,
         sums_ref,
         a_ref,
         b_ref,
@@ -387,10 +397,15 @@
     )
 
 
+def first_rest_kernel(f_ref, ya_ref, yb_ref, fs_ref):
+    rim = spread_edges(ya_ref, yb_ref)
+    stream_rest(lambda i, r: (f_ref[i, r], rim("f", i, r)), fs_ref)
+
+
 def middle_kernel(
     hs_ref, fs_ref, sums_ref, s_ref, ra_ref, rb_ref,
-    a_ref, b_ref, hs2_ref, fs2_ref, sums2_ref,
-    h1_ref, f1_ref, got_ref, phi_ref, grad_ref,
+    a_ref, b_ref, hs2_ref, sums2_ref, f1_ref,
+    h1_ref, got_ref, phi_ref, grad_ref,
 ):
     def new_h(r, t, zs, i, value):
         h1_ref[i, r, t, zs] = value
@@ -414,7 +429,6 @@
         lambda i, r: (h1_ref[i, r, 0], h1_ref[i, r, 1]),
         lambda i, r: (f1_ref[i, r, 0], f1_ref[i, r, 1]),
         hs2_ref,
-        fs2_ref,
         sums2_ref,
         a_ref,
         b_ref,
@@ -422,16 +436,29 @@
     )
 
 
+def middle_rest_kernel(f1_ref, fs_ref):
+    stream_rest(lambda i, r: (f1_ref[i, r, 0], f1_ref[i, r, 1]), fs_ref)
+
+
 def last_kernel(
     hs_ref, fs_ref, sums_ref, s_ref, ra_ref, rb_ref,
-    h_ref, f_ref,
-    got_ref, phi_ref, grad_ref,
+    h_hbm, f_hbm,
+    h_ref, f_ref, got_ref, phi_ref, grad_ref, sems,
 ):
     def new_h(r, t, zs, i, value):
-        h_ref[i, r, zs] = value
+        h_ref[r, i, zs] = value
 
     def new_f(r, t, zs, i, value):
-        f_ref[i, r, zs] = value
+        f_ref[r, i, zs] = value
+
+    copies = []
+
+    def row_done(r):
+        for n, (source, target) in enumerate(((h_ref, h_hbm), (f_ref, f_hbm))):
+            copies.append(
+                pltpu.make_async_copy(source.at[r], target.at[:, r], sems.at[r, n])
+            )
+            copies[-1].start()
 
     collide(
         hs_ref,
@@ -444,75 +471,86 @@
         new_f,
         (got_ref, phi_ref, grad_ref),
         1,
-    )
-
-
-def call(kernel, outs, *args, scratch=()):
-    spec = pl.BlockSpec(memory_space=pltpu.VMEM)
+        row_done,
+    )
+    for copy in copies:
+        copy.wait()
+
+
+HBM = pl.BlockSpec(memory_space=pltpu.HBM)
+VMEM = pl.BlockSpec(memory_space=pltpu.VMEM)
+TILE = (16, 128)
+COVER = pl.CostEstimate(flops=2_000_000_000, bytes_accessed=4_000_000, transcendentals=0)
+LIMIT = 16 * 1024 * 1024
+NEAR_Y, FAR_Y, NEAR_X, FAR_X = True, False, True, False
+
+
+def call(kernel, outs, *args, scratch=(), sems=None, source=VMEM, target=VMEM, cost=None):
+    kept = [pltpu.VMEM(shape, F32) for shape in scratch]
+    if sems is not None:
+        kept.append(pltpu.SemaphoreType.DMA(sems))
     return pl.pallas_call(
         kernel,
-        out_shape=[jax.ShapeDtypeStruct(shape, F32) for shape in outs],
-        in_specs=[spec] * len(args),
-        out_specs=[spec] * len(outs),
-        scratch_shapes=[pltpu.VMEM(shape, F32) for shape in scratch],
+        out_shape=[
+            out if hasattr(out, "dtype") else jax.ShapeDtypeStruct(out, F32)
+            for out in outs
+        ],
+        in_specs=[source] * len(args),
+        out_specs=[target] * len(outs),
+        scratch_shapes=kept,
         compiler_params=pltpu.CompilerParams(vmem_limit_bytes=LIMIT),
+        cost_estimate=cost,
     )(*args)
 
 
-def swap_near(block, axis):
-    return lax.ppermute(block, axis, [(i, i ^ 1) for i in range(lax.axis_size(axis))])
-
-
-def swap_far(block, axis):
+def swap_near(block, axis, gather):
     n = lax.axis_size(axis)
+    if gather:
+        groups = [[i, i + 1] for i in range(0, n, 2)]
+        return lax.all_gather(block, axis, axis_index_groups=groups)
+    return lax.ppermute(block, axis, [(i, i ^ 1) for i in range(n)])
+
+
+def swap_far(block, axis, gather):
+    n = lax.axis_size(axis)
+    if gather:
+        groups = [[i, (i + 1) % n] for i in range(1, n, 2)]
+        return lax.all_gather(block, axis, axis_index_groups=groups)
     route = [(i, (i + 1) % n if i % 2 else (i - 1) % n) for i in range(n)]
     return lax.ppermute(block, axis, route)
 
 
-TILE = (16, 128)
-LIMIT = 16 * 1024 * 1024
-
-
 def shards(phase_pops, flow_pops, solid_flags):
     edge, sent = (EDGE_TILES, *TILE), (SENT + 1, *TILE)
-    a, b = call(edges_kernel, [edge, edge], phase_pops, flow_pops, solid_flags)
-    a, b = swap_near(a, "gy"), swap_far(b, "gy")
     wide_h, wide_f = (NH, 2, 2, *TILE), (NF, 2, 2, *TILE)
     sums = (2, 2, *TILE)
     scratch = [(2, SENT, 2, *TILE), (4, 2, *TILE), (2, 2, 4, *TILE)]
-    a, b, hs, fs, kept, solid = call(
-        first_kernel,
-        [sent, sent, wide_h, wide_f, sums, (2, 2, *TILE)],
-        phase_pops,
-        flow_pops,
-        solid_flags,
-        a,
-        b,
-    )
-    a, b = swap_near(a, "gx"), swap_far(b, "gx")
-    a, b, hs, fs, kept = call(
+    h, f = phase_pops, flow_pops
+    (slot,) = call(slots_kernel, [jax.ShapeDtypeStruct(TILE, jnp.int32)], cost=COVER)
+    a, b = call(edges_kernel, [edge, edge], slot, h, f, solid_flags)
+    ya, yb = swap_near(a, "gy", NEAR_Y), swap_far(b, "gy", FAR_Y)
+    a, b, hs, kept, solid = call(
+        first_kernel, [sent, sent, wide_h, sums, (2, 2, *TILE)], h, f, solid_flags, ya, yb
+    )
+    a, b = swap_near(a, "gx", NEAR_X), swap_far(b, "gx", FAR_X)
+    (fs,) = call(first_rest_kernel, [wide_f], f, ya, yb)
+    a, b, hs, kept, f = call(
         middle_kernel,
-        [sent, sent, wide_h, (NF, 2, 1, *TILE), sums],
-        hs,
-        fs,
-        kept,
-        solid,
-        a,
-        b,
-        scratch=[wide_h, wide_f, *scratch],
-    )
-    a, b = swap_near(a, "gx"), swap_far(b, "gx")
+        [sent, sent, wide_h, sums, wide_f],
+        *(hs, fs, kept, solid, a, b),
+        scratch=[wide_h, *scratch],
+    )
+    a, b = swap_near(a, "gx", NEAR_X), swap_far(b, "gx", FAR_X)
+    (fs,) = call(middle_rest_kernel, [(NF, 2, 1, *TILE)], f)
+    out_h, out_f = (NH, 2, *TILE), (NF, 2, *TILE)
     return tuple(
         call(
             last_kernel,
-            [(NH, 2, *TILE), (NF, 2, *TILE)],
-            hs,
-            fs,
-            kept,
-            solid,
-            a,
-            b,
-            scratch=scratch,
+            [out_h, out_f],
+            *(hs, fs, kept, solid, a, b),
+            scratch=[(2, NH, *TILE), (2, NF, *TILE), *scratch],
+            sems=(2, 2),
+            target=HBM,
         )
     )
 

time: 54.3 us -> 46.1 us (0.85)
  the two profiles are of different devices: /device:TPU:32 before, /device:TPU:1 now
where the time goes in v2:
time: 46.1 us; the launch traced here: 45.9 us
  starting transfers between devices  24.2 us (52%)
  blocking collectives  17 us (37%)
  Pallas kernels  2.92 us (6%)
  local copies, waits for them, and re-layouts  1.02 us (2%)
  between operations  0.72 us (2%)
    ppermute x3, starting transfers between devices, swap_far(): return lax.ppermute(block, axis, route)  24.2 us
    all_gather x3, blocking collectives, swap_near(): return lax.all_gather(block, axis, axis_index_groups=groups)  17 us
    pallas_call x7, Pallas kernels, call(): pl.pallas_call(kernel, out_shape=[out if hasattr(out, 'dtype') else jax.S...  2.92 us
    unnamed x6, local copies, waits for them, and re-layouts  1.02 us
  transfers between devices with their start and end apart: 3, of which 0 were waited for; matrix products, arithmetic and copies ran while one was open for 0% of the time, Pallas kernels for 1%

profile of v2, /device:TPU:1, one launch (start us, length us, event | category | flops | bytes accessed | tf_op | source)
XLA Modules:
  0.0 45.9 jit_solution(9559525596502581115)
XLA Ops:
  0.6 0.0 copy-start
  0.6 0.0 copy-start.2
  0.6 0.0 copy-start.1
  0.7 0.9 %copy-done = f32[19,2,16,128]{3,2,1,0:T(8,128)S(1)} copy-done((f32[19,2,16,128]{3,2,1,0:T(8,128)S(1)}, f32[19,2,16,128]{3,2,1,0:T(8,128)}, u32[]{:S(2)}) %copy-start) | copy-done | bytes 311320
  1.6 0.0 copy-done.2
  1.6 0.1 copy-done.1
  1.7 0.3 shard_map.51
  2.0 9.0 %collective-permute-start = (f32[3,16,128]{2,1,0:T(8,128)S(1)}, f32[3,16,128]{2,1,0:T(8,128)S(1)}, u32[]{:S(2)}, u32[]{:S(2)}) collective-permute-start(f32[3,16,128]{2,1,0:T(8,128)S(1)} %get-tuple-element.15), channel_id=1, source_target_pairs={{0,7},{1,2},{2,1},{3,4},{4,3},{5,6},{6,5},{7,0},{8,15},{9,10},{10,... | collective-permute-start | bytes 73736 | tf_op jit(solution)/shard_map/ppermute | solution.py:520
  11.0 8.0 %all-gather = f32[6,16,128]{2,1,0:T(8,128)S(1)} all-gather(f32[3,16,128]{2,1,0:T(8,128)S(1)} %get-tuple-element.14), channel_id=2, replica_groups={{0,1},{2,3},{4,5},{6,7},{8,9},{10,11},{12,13},{14,15},{16,17},{18,19},{..., dimensions={0}, use_global_device_ids=true | all-gather | bytes 73728 | tf_op jit(solution)/shard_map/all_gather | solution.py:510
  19.0 0.0 collective-permute-done.yb_ref
  19.0 0.4 shard_map.52
  19.4 9.1 %collective-permute-start.1 = (f32[12,16,128]{2,1,0:T(8,128)S(1)}, f32[12,16,128]{2,1,0:T(8,128)S(1)}, u32[]{:S(2)}, u32[]{:S(2)}) collective-permute-start(f32[12,16,128]{2,1,0:T(8,128)S(1)} %get-tuple-element.20), channel_id=1, source_target_pairs={{0,760},{8,16},{16,8},{24,32},{32,24},{40,48},{48,40},{56,64},{64,... | collective-permute-start | bytes 294920 | tf_op jit(solution)/shard_map/ppermute | solution.py:520
  28.5 0.3 shard_map.53.fs_ref
  28.8 4.4 %all-gather.1 = f32[24,16,128]{2,1,0:T(8,128)S(1)} all-gather(f32[12,16,128]{2,1,0:T(8,128)S(1)} %get-tuple-element.19), channel_id=3, replica_groups={{0,8},{16,24},{32,40},{48,56},{64,72},{80,88},{96,104},{112,120},{128,1..., dimensions={0}, use_global_device_ids=true | all-gather | bytes 294912 | tf_op jit(solution)/shard_map/all_gather | solution.py:510
  33.2 0.0 collective-permute-done.1.rb_ref
  33.2 0.7 %shard_map.54 = (f32[12,16,128]{2,1,0:T(8,128)S(1)}, f32[12,16,128]{2,1,0:T(8,128)S(1)}, f32[15,2,2,16,128]{4,3,2,1,0:T(8,128)S(1)}, f32[2,2,16,128]{3,2,1,0:T(8,128)S(1)}, f32[19,2,2,16,128]{4,3,2,1,0:T(8,128)S(1)}) custom-call(f32[15,2,2,16,128]{4,3,2,1,0:T(8,128)S(1)} %get-tuple-element.16.hs_ref, f32[19,2,2,16,128]{4,3,2,1,0:T(8,128)S(1)} %shard_map.53.fs_ref, ...), custom_call_target="tpu_custom_call" | custom-call | tf_op jit(solution)/shard_map/pallas_call | solution.py:492
  33.9 6.1 %collective-permute-start.2 = (f32[12,16,128]{2,1,0:T(8,128)S(1)}, f32[12,16,128]{2,1,0:T(8,128)S(1)}, u32[]{:S(2)}, u32[]{:S(2)}) collective-permute-start(f32[12,16,128]{2,1,0:T(8,128)S(1)} %get-tuple-element.25), channel_id=1, source_target_pairs={{0,760},{8,16},{16,8},{24,32},{32,24},{40,48},{48,40},{56,64},{64,... | collective-permute-start | bytes 294920 | tf_op jit(solution)/shard_map/ppermute | solution.py:520
  40.1 0.1 shard_map.55.fs_ref
  40.2 4.5 %all-gather.2 = f32[24,16,128]{2,1,0:T(8,128)S(1)} all-gather(f32[12,16,128]{2,1,0:T(8,128)S(1)} %get-tuple-element.24), channel_id=4, replica_groups={{0,8},{16,24},{32,40},{48,56},{64,72},{80,88},{96,104},{112,120},{128,1..., dimensions={0}, use_global_device_ids=true | all-gather | bytes 294912 | tf_op jit(solution)/shard_map/all_gather | solution.py:510
  44.8 0.0 collective-permute-done.2.rb_ref
  44.8 1.1 %shard_map.56 = (f32[15,2,16,128]{3,2,1,0:T(8,128)}, f32[19,2,16,128]{3,2,1,0:T(8,128)}) custom-call(f32[15,2,2,16,128]{4,3,2,1,0:T(8,128)S(1)} %get-tuple-element.21.hs_ref, f32[19,2,1,16,128]{4,3,2,1,0:T(8,128)S(1)} %shard_map.55.fs_ref, f32[2,2,16,128]{3,2,1,0:T(8,128)S(1)} %get-tuple-element.23.sums_ref, f32[2,2,16,128]{3,2,1,0:T(8,128)S(1)} %get-tuple-element.18.s_ref, ...), custom_call_target="tpu_custom_call" | custom-call | tf_op jit(solution)/shard_map/pallas_call | solution.py:492
  (1 shorter events, 0.0 us)
Async XLA Ops:
  0.6 1.0 %copy-start = (f32[19,2,16,128]{3,2,1,0:T(8,128)S(1)}, f32[19,2,16,128]{3,2,1,0:T(8,128)}, u32[]{:S(2)}) copy-start(f32[19,2,16,128]{3,2,1,0:T(8,128)} %f_ref.5) | copy-start | bytes 933892
  0.6 1.0 %copy-start.2 = (s32[2,16,128]{2,1,0:T(8,128)S(1)}, s32[2,16,128]{2,1,0:T(8,128)}, u32[]{:S(2)}) copy-start(s32[2,16,128]{2,1,0:T(8,128)} %s_ref.3) | copy-start | bytes 49156
  0.6 1.0 %copy-start.1 = (f32[15,2,16,128]{3,2,1,0:T(8,128)S(1)}, f32[15,2,16,128]{3,2,1,0:T(8,128)}, u32[]{:S(2)}) copy-start(f32[15,2,16,128]{3,2,1,0:T(8,128)} %h_ref.3) | copy-start | bytes 737284
  2.0 17.0 %collective-permute-start = (f32[3,16,128]{2,1,0:T(8,128)S(1)}, f32[3,16,128]{2,1,0:T(8,128)S(1)}, u32[]{:S(2)}, u32[]{:S(2)}) collective-permute-start(f32[3,16,128]{2,1,0:T(8,128)S(1)} %get-tuple-element.15), channel_id=1, source_target_pairs={{0,7},{1,2},{2,1},{3,4},{4,3},{5,6},{6,5},{7,0},{8,15},{9,10},{10,... | collective-permute-start | bytes 73736 | tf_op jit(solution)/shard_map/ppermute | solution.py:520
  19.4 13.8 %collective-permute-start.1 = (f32[12,16,128]{2,1,0:T(8,128)S(1)}, f32[12,16,128]{2,1,0:T(8,128)S(1)}, u32[]{:S(2)}, u32[]{:S(2)}) collective-permute-start(f32[12,16,128]{2,1,0:T(8,128)S(1)} %get-tuple-element.20), channel_id=1, source_target_pairs={{0,760},{8,16},{16,8},{24,32},{32,24},{40,48},{48,40},{56,64},{64,... | collective-permute-start | bytes 294920 | tf_op jit(solution)/shard_map/ppermute | solution.py:520
  33.9 10.8 %collective-permute-start.2 = (f32[12,16,128]{2,1,0:T(8,128)S(1)}, f32[12,16,128]{2,1,0:T(8,128)S(1)}, u32[]{:S(2)}, u32[]{:S(2)}) collective-permute-start(f32[12,16,128]{2,1,0:T(8,128)S(1)} %get-tuple-element.25), channel_id=1, source_target_pairs={{0,760},{8,16},{16,8},{24,32},{32,24},{40,48},{48,40},{56,64},{64,... | collective-permute-start | bytes 294920 | tf_op jit(solution)/shard_map/ppermute | solution.py:520

commit v3 on v2

--- a/solution.py
+++ b/solution.py
@@ -482,7 +482,7 @@
 TILE = (16, 128)
 COVER = pl.CostEstimate(flops=2_000_000_000, bytes_accessed=4_000_000, transcendentals=0)
 LIMIT = 16 * 1024 * 1024
-NEAR_Y, FAR_Y, NEAR_X, FAR_X = True, False, True, False
+NEAR_Y, FAR_Y, NEAR_X, FAR_X = True, True, True, False
 
 
 def call(kernel, outs, *args, scratch=(), sems=None, source=VMEM, target=VMEM, cost=None):

time: 46.1 us -> 46.1 us (level)
  the two profiles are of different devices: /device:TPU:1 before, /device:TPU:192 now
where the time goes in v3:
time: 46.1 us; the launch traced here: 45.9 us
  blocking collectives  23.7 us (51%)
  starting transfers between devices  17.6 us (38%)
  Pallas kernels  2.92 us (6%)
  local copies, waits for them, and re-layouts  1.02 us (2%)
  between operations  0.71 us (2%)
    ppermute x2, starting transfers between devices, swap_far(): return lax.ppermute(block, axis, route)  17.6 us
    all_gather x3, blocking collectives, swap_near(): return lax.all_gather(block, axis, axis_index_groups=groups)  14.8 us
    all_gather x1, blocking collectives, swap_far(): return lax.all_gather(block, axis, axis_index_groups=groups)  8.84 us
    pallas_call x7, Pallas kernels, call(): pl.pallas_call(kernel, out_shape=[out if hasattr(out, 'dtype') else jax.S...  2.92 us
    unnamed x6, local copies, waits for them, and re-layouts  1.02 us
  transfers between devices with their start and end apart: 2, of which 0 were waited for; matrix products, arithmetic and copies ran while one was open for 0% of the time, Pallas kernels for 1%

profile of v3, /device:TPU:192, one launch (start us, length us, event | category | flops | bytes accessed | tf_op | source)
XLA Modules:
  0.0 45.9 jit_solution(11172716010498614798)
XLA Ops:
  0.6 0.0 copy-start
  0.6 0.0 copy-start.2
  0.6 0.0 copy-start.1
  0.7 0.9 %copy-done = f32[19,2,16,128]{3,2,1,0:T(8,128)S(1)} copy-done((f32[19,2,16,128]{3,2,1,0:T(8,128)S(1)}, f32[19,2,16,128]{3,2,1,0:T(8,128)}, u32[]{:S(2)}) %copy-start) | copy-done | bytes 311320
  1.6 0.0 copy-done.2
  1.6 0.1 copy-done.1
  1.7 0.3 shard_map.51
  2.0 1.8 %all-gather = f32[6,16,128]{2,1,0:T(8,128)S(1)} all-gather(f32[3,16,128]{2,1,0:T(8,128)S(1)} %get-tuple-element.14), channel_id=2, replica_groups={{0,1},{2,3},{4,5},{6,7},{8,9},{10,11},{12,13},{14,15},{16,17},{18,19},{..., dimensions={0}, use_global_device_ids=true | all-gather | bytes 73728 | tf_op jit(solution)/shard_map/all_gather | solution.py:510
  3.8 8.8 %all-gather.1 = f32[6,16,128]{2,1,0:T(8,128)S(1)} all-gather(f32[3,16,128]{2,1,0:T(8,128)S(1)} %get-tuple-element.15), channel_id=3, replica_groups={{1,2},{3,4},{5,6},{7,0},{9,10},{11,12},{13,14},{15,8},{17,18},{19,20},{..., dimensions={0}, use_global_device_ids=true | all-gather | bytes 73728 | tf_op jit(solution)/shard_map/all_gather | solution.py:518
  12.6 0.4 shard_map.52
  13.0 10.5 %collective-permute-start = (f32[12,16,128]{2,1,0:T(8,128)S(1)}, f32[12,16,128]{2,1,0:T(8,128)S(1)}, u32[]{:S(2)}, u32[]{:S(2)}) collective-permute-start(f32[12,16,128]{2,1,0:T(8,128)S(1)} %get-tuple-element.20), channel_id=1, source_target_pairs={{0,760},{8,16},{16,8},{24,32},{32,24},{40,48},{48,40},{56,64},{64,... | collective-permute-start | bytes 294920 | tf_op jit(solution)/shard_map/ppermute | solution.py:520
  23.5 0.3 shard_map.53.fs_ref
  23.8 6.5 %all-gather.2 = f32[24,16,128]{2,1,0:T(8,128)S(1)} all-gather(f32[12,16,128]{2,1,0:T(8,128)S(1)} %get-tuple-element.19), channel_id=4, replica_groups={{0,8},{16,24},{32,40},{48,56},{64,72},{80,88},{96,104},{112,120},{128,1..., dimensions={0}, use_global_device_ids=true | all-gather | bytes 294912 | tf_op jit(solution)/shard_map/all_gather | solution.py:510
  30.3 0.0 collective-permute-done.rb_ref
  30.3 0.7 %shard_map.54 = (f32[12,16,128]{2,1,0:T(8,128)S(1)}, f32[12,16,128]{2,1,0:T(8,128)S(1)}, f32[15,2,2,16,128]{4,3,2,1,0:T(8,128)S(1)}, f32[2,2,16,128]{3,2,1,0:T(8,128)S(1)}, f32[19,2,2,16,128]{4,3,2,1,0:T(8,128)S(1)}) custom-call(f32[15,2,2,16,128]{4,3,2,1,0:T(8,128)S(1)} %get-tuple-element.16.hs_ref, f32[19,2,2,16,128]{4,3,2,1,0:T(8,128)S(1)} %shard_map.53.fs_ref, ...), custom_call_target="tpu_custom_call" | custom-call | tf_op jit(solution)/shard_map/pallas_call | solution.py:492
  31.0 7.1 %collective-permute-start.1 = (f32[12,16,128]{2,1,0:T(8,128)S(1)}, f32[12,16,128]{2,1,0:T(8,128)S(1)}, u32[]{:S(2)}, u32[]{:S(2)}) collective-permute-start(f32[12,16,128]{2,1,0:T(8,128)S(1)} %get-tuple-element.25), channel_id=1, source_target_pairs={{0,760},{8,16},{16,8},{24,32},{32,24},{40,48},{48,40},{56,64},{64,... | collective-permute-start | bytes 294920 | tf_op jit(solution)/shard_map/ppermute | solution.py:520
  38.2 0.1 shard_map.55.fs_ref
  38.3 6.5 %all-gather.3 = f32[24,16,128]{2,1,0:T(8,128)S(1)} all-gather(f32[12,16,128]{2,1,0:T(8,128)S(1)} %get-tuple-element.24), channel_id=5, replica_groups={{0,8},{16,24},{32,40},{48,56},{64,72},{80,88},{96,104},{112,120},{128,1..., dimensions={0}, use_global_device_ids=true | all-gather | bytes 294912 | tf_op jit(solution)/shard_map/all_gather | solution.py:510
  44.8 0.0 collective-permute-done.1.rb_ref
  44.8 1.1 %shard_map.56 = (f32[15,2,16,128]{3,2,1,0:T(8,128)}, f32[19,2,16,128]{3,2,1,0:T(8,128)}) custom-call(f32[15,2,2,16,128]{4,3,2,1,0:T(8,128)S(1)} %get-tuple-element.21.hs_ref, f32[19,2,1,16,128]{4,3,2,1,0:T(8,128)S(1)} %shard_map.55.fs_ref, f32[2,2,16,128]{3,2,1,0:T(8,128)S(1)} %get-tuple-element.23.sums_ref, f32[2,2,16,128]{3,2,1,0:T(8,128)S(1)} %get-tuple-element.18.s_ref, ...), custom_call_target="tpu_custom_call" | custom-call | tf_op jit(solution)/shard_map/pallas_call | solution.py:492
  (1 shorter events, 0.0 us)
Async XLA Ops:
  0.6 1.0 %copy-start = (f32[19,2,16,128]{3,2,1,0:T(8,128)S(1)}, f32[19,2,16,128]{3,2,1,0:T(8,128)}, u32[]{:S(2)}) copy-start(f32[19,2,16,128]{3,2,1,0:T(8,128)} %f_ref.5) | copy-start | bytes 933892
  0.6 1.0 %copy-start.2 = (s32[2,16,128]{2,1,0:T(8,128)S(1)}, s32[2,16,128]{2,1,0:T(8,128)}, u32[]{:S(2)}) copy-start(s32[2,16,128]{2,1,0:T(8,128)} %s_ref.3) | copy-start | bytes 49156
  0.6 1.0 %copy-start.1 = (f32[15,2,16,128]{3,2,1,0:T(8,128)S(1)}, f32[15,2,16,128]{3,2,1,0:T(8,128)}, u32[]{:S(2)}) copy-start(f32[15,2,16,128]{3,2,1,0:T(8,128)} %h_ref.3) | copy-start | bytes 737284
  13.0 17.3 %collective-permute-start = (f32[12,16,128]{2,1,0:T(8,128)S(1)}, f32[12,16,128]{2,1,0:T(8,128)S(1)}, u32[]{:S(2)}, u32[]{:S(2)}) collective-permute-start(f32[12,16,128]{2,1,0:T(8,128)S(1)} %get-tuple-element.20), channel_id=1, source_target_pairs={{0,760},{8,16},{16,8},{24,32},{32,24},{40,48},{48,40},{56,64},{64,... | collective-permute-start | bytes 294920 | tf_op jit(solution)/shard_map/ppermute | solution.py:520
  31.0 13.7 %collective-permute-start.1 = (f32[12,16,128]{2,1,0:T(8,128)S(1)}, f32[12,16,128]{2,1,0:T(8,128)S(1)}, u32[]{:S(2)}, u32[]{:S(2)}) collective-permute-start(f32[12,16,128]{2,1,0:T(8,128)S(1)} %get-tuple-element.25), channel_id=1, source_target_pairs={{0,760},{8,16},{16,8},{24,32},{32,24},{40,48},{48,40},{56,64},{64,... | collective-permute-start | bytes 294920 | tf_op jit(solution)/shard_map/ppermute | solution.py:520

commit v4 on v3

--- a/solution.py
+++ b/solution.py
@@ -397,16 +397,14 @@
     )
 
 
-def first_rest_kernel(f_ref, ya_ref, yb_ref, fs_ref):
+def middle_kernel(
+    hs_ref, f_ref, ya_ref, yb_ref, sums_ref, s_ref, ra_ref, rb_ref,
+    a_ref, b_ref, hs2_ref, sums2_ref, f1_ref,
+    h1_ref, fs_ref, got_ref, phi_ref, grad_ref,
+):
     rim = spread_edges(ya_ref, yb_ref)
     stream_rest(lambda i, r: (f_ref[i, r], rim("f", i, r)), fs_ref)
 
-
-def middle_kernel(
-    hs_ref, fs_ref, sums_ref, s_ref, ra_ref, rb_ref,
-    a_ref, b_ref, hs2_ref, sums2_ref, f1_ref,
-    h1_ref, got_ref, phi_ref, grad_ref,
-):
     def new_h(r, t, zs, i, value):
         h1_ref[i, r, t, zs] = value
 
@@ -436,15 +434,13 @@
     )
 
 
-def middle_rest_kernel(f1_ref, fs_ref):
+def last_kernel(
+    hs_ref, f1_ref, sums_ref, s_ref, ra_ref, rb_ref,
+    h_hbm, f_hbm,
+    h_ref, f_ref, fs_ref, got_ref, phi_ref, grad_ref, sems,
+):
     stream_rest(lambda i, r: (f1_ref[i, r, 0], f1_ref[i, r, 1]), fs_ref)
 
-
-def last_kernel(
-    hs_ref, fs_ref, sums_ref, s_ref, ra_ref, rb_ref,
-    h_hbm, f_hbm,
-    h_ref, f_ref, got_ref, phi_ref, grad_ref, sems,
-):
     def new_h(r, t, zs, i, value):
         h_ref[r, i, zs] = value
 
@@ -533,22 +529,20 @@
         first_kernel, [sent, sent, wide_h, sums, (2, 2, *TILE)], h, f, solid_flags, ya, yb
     )
     a, b = swap_near(a, "gx", NEAR_X), swap_far(b, "gx", FAR_X)
-    (fs,) = call(first_rest_kernel, [wide_f], f, ya, yb)
     a, b, hs, kept, f = call(
         middle_kernel,
         [sent, sent, wide_h, sums, wide_f],
-        *(hs, fs, kept, solid, a, b),
-        scratch=[wide_h, *scratch],
+        *(hs, f, ya, yb, kept, solid, a, b),
+        scratch=[wide_h, wide_f, *scratch],
     )
     a, b = swap_near(a, "gx", NEAR_X), swap_far(b, "gx", FAR_X)
-    (fs,) = call(middle_rest_kernel, [(NF, 2, 1, *TILE)], f)
     out_h, out_f = (NH, 2, *TILE), (NF, 2, *TILE)
     return tuple(
         call(
             last_kernel,
             [out_h, out_f],
-            *(hs, fs, kept, solid, a, b),
-            scratch=[(2, NH, *TILE), (2, NF, *TILE), *scratch],
+            *(hs, f, kept, solid, a, b),
+            scratch=[(2, NH, *TILE), (2, NF, *TILE), (NF, 2, 1, *TILE), *scratch],
             sems=(2, 2),
             target=HBM,
         )

time: 46.1 us -> 46.2 us (level)
    pallas_call x7 -> x5, Pallas kernels: 2.92 us -> 2.7 us  [call(): pl.pallas_call(kernel, out_shape=[out if hasattr(out, 'dtype') else jax.S...]
  transfers between devices with their start and end apart: 2 -> 2, of which waited for: 0 -> 0; matrix products, arithmetic and copies ran while one was open for 0% -> 0% of each run, Pallas kernels for 1% -> 0%
where the time goes in v4:
time: 46.2 us; the launch traced here: 45.9 us
  blocking collectives  23.7 us (51%)
  starting transfers between devices  17.9 us (39%)
  Pallas kernels  2.7 us (6%)
  local copies, waits for them, and re-layouts  1.02 us (2%)
  between operations  0.69 us (1%)
    ppermute x2, starting transfers between devices, swap_far(): return lax.ppermute(block, axis, route)  17.9 us
    all_gather x3, blocking collectives, swap_near(): return lax.all_gather(block, axis, axis_index_groups=groups)  14.8 us
    all_gather x1, blocking collectives, swap_far(): return lax.all_gather(block, axis, axis_index_groups=groups)  8.84 us
    pallas_call x5, Pallas kernels, call(): pl.pallas_call(kernel, out_shape=[out if hasattr(out, 'dtype') else jax.S...  2.7 us
    unnamed x6, local copies, waits for them, and re-layouts  1.02 us
  transfers between devices with their start and end apart: 2, of which 0 were waited for; matrix products, arithmetic and copies ran while one was open for 0% of the time, Pallas kernels for 0%

profile of v4, /device:TPU:192, one launch (start us, length us, event | category | flops | bytes accessed | tf_op | source)
XLA Modules:
  0.0 45.9 jit_solution(15936744459863595090)
XLA Ops:
  0.6 0.0 copy-start
  0.6 0.0 copy-start.2
  0.6 0.0 copy-start.1
  0.7 0.9 %copy-done = f32[19,2,16,128]{3,2,1,0:T(8,128)S(1)} copy-done((f32[19,2,16,128]{3,2,1,0:T(8,128)S(1)}, f32[19,2,16,128]{3,2,1,0:T(8,128)}, u32[]{:S(2)}) %copy-start) | copy-done | bytes 311320
  1.6 0.0 copy-done.2
  1.6 0.1 copy-done.1
  1.7 0.3 shard_map.51
  2.0 1.8 %all-gather = f32[6,16,128]{2,1,0:T(8,128)S(1)} all-gather(f32[3,16,128]{2,1,0:T(8,128)S(1)} %get-tuple-element.14), channel_id=2, replica_groups={{0,1},{2,3},{4,5},{6,7},{8,9},{10,11},{12,13},{14,15},{16,17},{18,19},{..., dimensions={0}, use_global_device_ids=true | all-gather | bytes 73728 | tf_op jit(solution)/shard_map/all_gather | solution.py:506
  3.8 8.8 %all-gather.1 = f32[6,16,128]{2,1,0:T(8,128)S(1)} all-gather(f32[3,16,128]{2,1,0:T(8,128)S(1)} %get-tuple-element.15), channel_id=3, replica_groups={{1,2},{3,4},{5,6},{7,0},{9,10},{11,12},{13,14},{15,8},{17,18},{19,20},{..., dimensions={0}, use_global_device_ids=true | all-gather | bytes 73728 | tf_op jit(solution)/shard_map/all_gather | solution.py:514
  12.6 0.4 shard_map.52
  13.0 10.5 %collective-permute-start = (f32[12,16,128]{2,1,0:T(8,128)S(1)}, f32[12,16,128]{2,1,0:T(8,128)S(1)}, u32[]{:S(2)}, u32[]{:S(2)}) collective-permute-start(f32[12,16,128]{2,1,0:T(8,128)S(1)} %get-tuple-element.20), channel_id=1, source_target_pairs={{0,760},{8,16},{16,8},{24,32},{32,24},{40,48},{48,40},{56,64},{64,... | collective-permute-start | bytes 294920 | tf_op jit(solution)/shard_map/ppermute | solution.py:516
  23.5 6.5 %all-gather.2 = f32[24,16,128]{2,1,0:T(8,128)S(1)} all-gather(f32[12,16,128]{2,1,0:T(8,128)S(1)} %get-tuple-element.19), channel_id=4, replica_groups={{0,8},{16,24},{32,40},{48,56},{64,72},{80,88},{96,104},{112,120},{128,1..., dimensions={0}, use_global_device_ids=true | all-gather | bytes 294912 | tf_op jit(solution)/shard_map/all_gather | solution.py:506
  30.0 0.0 collective-permute-done.rb_ref
  30.0 0.9 %shard_map.53 = (f32[12,16,128]{2,1,0:T(8,128)S(1)}, f32[12,16,128]{2,1,0:T(8,128)S(1)}, f32[15,2,2,16,128]{4,3,2,1,0:T(8,128)S(1)}, f32[2,2,16,128]{3,2,1,0:T(8,128)S(1)}, f32[19,2,2,16,128]{4,3,2,1,0:T(8,128)S(1)}) custom-call(f32[15,2,2,16,128]{4,3,2,1,0:T(8,128)S(1)} %get-tuple-element.16.hs_ref, f32[19,2,16,128]{3,2,1,0:T(8,128)S(1)} %copy-done, ...), custom_call_target="tpu_custom_call" | custom-call | tf_op jit(solution)/shard_map/pallas_call | solution.py:488
  30.9 7.4 %collective-permute-start.1 = (f32[12,16,128]{2,1,0:T(8,128)S(1)}, f32[12,16,128]{2,1,0:T(8,128)S(1)}, u32[]{:S(2)}, u32[]{:S(2)}) collective-permute-start(f32[12,16,128]{2,1,0:T(8,128)S(1)} %get-tuple-element.25), channel_id=1, source_target_pairs={{0,760},{8,16},{16,8},{24,32},{32,24},{40,48},{48,40},{56,64},{64,... | collective-permute-start | bytes 294920 | tf_op jit(solution)/shard_map/ppermute | solution.py:516
  38.3 6.5 %all-gather.3 = f32[24,16,128]{2,1,0:T(8,128)S(1)} all-gather(f32[12,16,128]{2,1,0:T(8,128)S(1)} %get-tuple-element.24), channel_id=5, replica_groups={{0,8},{16,24},{32,40},{48,56},{64,72},{80,88},{96,104},{112,120},{128,1..., dimensions={0}, use_global_device_ids=true | all-gather | bytes 294912 | tf_op jit(solution)/shard_map/all_gather | solution.py:506
  44.8 0.0 collective-permute-done.1.rb_ref
  44.8 1.1 %shard_map.54 = (f32[15,2,16,128]{3,2,1,0:T(8,128)}, f32[19,2,16,128]{3,2,1,0:T(8,128)}) custom-call(f32[15,2,2,16,128]{4,3,2,1,0:T(8,128)S(1)} %get-tuple-element.21.hs_ref, f32[19,2,2,16,128]{4,3,2,1,0:T(8,128)S(1)} %get-tuple-element.22.f1_ref, f32[2,2,16,128]{3,2,1,0:T(8,128)S(1)} %get-tuple-element.23.sums_ref, ...), custom_call_target="tpu_custom_call" | custom-call | tf_op jit(solution)/shard_map/pallas_call | solution.py:488
  (1 shorter events, 0.0 us)
Async XLA Ops:
  0.6 1.0 %copy-start = (f32[19,2,16,128]{3,2,1,0:T(8,128)S(1)}, f32[19,2,16,128]{3,2,1,0:T(8,128)}, u32[]{:S(2)}) copy-start(f32[19,2,16,128]{3,2,1,0:T(8,128)} %f_ref.5) | copy-start | bytes 933892
  0.6 1.0 %copy-start.2 = (s32[2,16,128]{2,1,0:T(8,128)S(1)}, s32[2,16,128]{2,1,0:T(8,128)}, u32[]{:S(2)}) copy-start(s32[2,16,128]{2,1,0:T(8,128)} %s_ref.3) | copy-start | bytes 49156
  0.6 1.0 %copy-start.1 = (f32[15,2,16,128]{3,2,1,0:T(8,128)S(1)}, f32[15,2,16,128]{3,2,1,0:T(8,128)}, u32[]{:S(2)}) copy-start(f32[15,2,16,128]{3,2,1,0:T(8,128)} %h_ref.3) | copy-start | bytes 737284
  13.0 17.0 %collective-permute-start = (f32[12,16,128]{2,1,0:T(8,128)S(1)}, f32[12,16,128]{2,1,0:T(8,128)S(1)}, u32[]{:S(2)}, u32[]{:S(2)}) collective-permute-start(f32[12,16,128]{2,1,0:T(8,128)S(1)} %get-tuple-element.20), channel_id=1, source_target_pairs={{0,760},{8,16},{16,8},{24,32},{32,24},{40,48},{48,40},{56,64},{64,... | collective-permute-start | bytes 294920 | tf_op jit(solution)/shard_map/ppermute | solution.py:516
  30.9 13.9 %collective-permute-start.1 = (f32[12,16,128]{2,1,0:T(8,128)S(1)}, f32[12,16,128]{2,1,0:T(8,128)S(1)}, u32[]{:S(2)}, u32[]{:S(2)}) collective-permute-start(f32[12,16,128]{2,1,0:T(8,128)S(1)} %get-tuple-element.25), channel_id=1, source_target_pairs={{0,760},{8,16},{16,8},{24,32},{32,24},{40,48},{48,40},{56,64},{64,... | collective-permute-start | bytes 294920 | tf_op jit(solution)/shard_map/ppermute | solution.py:516

commit v5 on v4

--- a/solution.py
+++ b/solution.py
@@ -397,14 +397,16 @@
     )
 
 
-def middle_kernel(
-    hs_ref, f_ref, ya_ref, yb_ref, sums_ref, s_ref, ra_ref, rb_ref,
-    a_ref, b_ref, hs2_ref, sums2_ref, f1_ref,
-    h1_ref, fs_ref, got_ref, phi_ref, grad_ref,
-):
+def first_rest_kernel(f_ref, ya_ref, yb_ref, fs_ref):
     rim = spread_edges(ya_ref, yb_ref)
     stream_rest(lambda i, r: (f_ref[i, r], rim("f", i, r)), fs_ref)
 
+
+def middle_kernel(
+    hs_ref, fs_ref, sums_ref, s_ref, ra_ref, rb_ref,
+    a_ref, b_ref, hs2_ref, sums2_ref, f1_ref,
+    h1_ref, got_ref, phi_ref, grad_ref,
+):
     def new_h(r, t, zs, i, value):
         h1_ref[i, r, t, zs] = value
 
@@ -529,11 +531,12 @@
         first_kernel, [sent, sent, wide_h, sums, (2, 2, *TILE)], h, f, solid_flags, ya, yb
     )
     a, b = swap_near(a, "gx", NEAR_X), swap_far(b, "gx", FAR_X)
+    (fs,) = call(first_rest_kernel, [wide_f], f, ya, yb)
     a, b, hs, kept, f = call(
         middle_kernel,
         [sent, sent, wide_h, sums, wide_f],
-        *(hs, f, ya, yb, kept, solid, a, b),
-        scratch=[wide_h, wide_f, *scratch],
+        *(hs, fs, kept, solid, a, b),
+        scratch=[wide_h, *scratch],
     )
     a, b = swap_near(a, "gx", NEAR_X), swap_far(b, "gx", FAR_X)
     out_h, out_f = (NH, 2, *TILE), (NF, 2, *TILE)

time: 46.2 us -> 46 us (level)
    pallas_call x5 -> x6, Pallas kernels: 2.7 us -> 2.84 us  [call(): pl.pallas_call(kernel, out_shape=[out if hasattr(out, 'dtype') else jax.S...]
  transfers between devices with their start and end apart: 2 -> 2, of which waited for: 0 -> 0; matrix products, arithmetic and copies ran while one was open for 0% -> 0% of each run, Pallas kernels for 0% -> 1%
where the time goes in v5:
time: 46 us; the launch traced here: 45.8 us
  blocking collectives  23.7 us (52%)
  starting transfers between devices  17.6 us (38%)
  Pallas kernels  2.84 us (6%)
  local copies, waits for them, and re-layouts  1.02 us (2%)
  between operations  0.7 us (2%)
    ppermute x2, starting transfers between devices, swap_far(): return lax.ppermute(block, axis, route)  17.6 us
    all_gather x3, blocking collectives, swap_near(): return lax.all_gather(block, axis, axis_index_groups=groups)  14.8 us
    all_gather x1, blocking collectives, swap_far(): return lax.all_gather(block, axis, axis_index_groups=groups)  8.84 us
    pallas_call x6, Pallas kernels, call(): pl.pallas_call(kernel, out_shape=[out if hasattr(out, 'dtype') else jax.S...  2.84 us
    unnamed x6, local copies, waits for them, and re-layouts  1.02 us
  transfers between devices with their start and end apart: 2, of which 0 were waited for; matrix products, arithmetic and copies ran while one was open for 0% of the time, Pallas kernels for 1%

profile of v5, /device:TPU:192, one launch (start us, length us, event | category | flops | bytes accessed | tf_op | source)
XLA Modules:
  0.0 45.8 jit_solution(6288356940772219349)
XLA Ops:
  0.6 0.0 copy-start
  0.6 0.0 copy-start.2
  0.6 0.0 copy-start.1
  0.7 0.9 %copy-done = f32[19,2,16,128]{3,2,1,0:T(8,128)S(1)} copy-done((f32[19,2,16,128]{3,2,1,0:T(8,128)S(1)}, f32[19,2,16,128]{3,2,1,0:T(8,128)}, u32[]{:S(2)}) %copy-start) | copy-done | bytes 311320
  1.6 0.0 copy-done.2
  1.6 0.1 copy-done.1
  1.7 0.3 shard_map.51
  2.0 1.8 %all-gather = f32[6,16,128]{2,1,0:T(8,128)S(1)} all-gather(f32[3,16,128]{2,1,0:T(8,128)S(1)} %get-tuple-element.14), channel_id=2, replica_groups={{0,1},{2,3},{4,5},{6,7},{8,9},{10,11},{12,13},{14,15},{16,17},{18,19},{..., dimensions={0}, use_global_device_ids=true | all-gather | bytes 73728 | tf_op jit(solution)/shard_map/all_gather | solution.py:508
  3.8 8.8 %all-gather.1 = f32[6,16,128]{2,1,0:T(8,128)S(1)} all-gather(f32[3,16,128]{2,1,0:T(8,128)S(1)} %get-tuple-element.15), channel_id=3, replica_groups={{1,2},{3,4},{5,6},{7,0},{9,10},{11,12},{13,14},{15,8},{17,18},{19,20},{..., dimensions={0}, use_global_device_ids=true | all-gather | bytes 73728 | tf_op jit(solution)/shard_map/all_gather | solution.py:516
  12.6 0.4 shard_map.52
  13.0 10.5 %collective-permute-start = (f32[12,16,128]{2,1,0:T(8,128)S(1)}, f32[12,16,128]{2,1,0:T(8,128)S(1)}, u32[]{:S(2)}, u32[]{:S(2)}) collective-permute-start(f32[12,16,128]{2,1,0:T(8,128)S(1)} %get-tuple-element.20), channel_id=1, source_target_pairs={{0,760},{8,16},{16,8},{24,32},{32,24},{40,48},{48,40},{56,64},{64,... | collective-permute-start | bytes 294920 | tf_op jit(solution)/shard_map/ppermute | solution.py:518
  23.5 0.3 shard_map.53.fs_ref
  23.8 6.5 %all-gather.2 = f32[24,16,128]{2,1,0:T(8,128)S(1)} all-gather(f32[12,16,128]{2,1,0:T(8,128)S(1)} %get-tuple-element.19), channel_id=4, replica_groups={{0,8},{16,24},{32,40},{48,56},{64,72},{80,88},{96,104},{112,120},{128,1..., dimensions={0}, use_global_device_ids=true | all-gather | bytes 294912 | tf_op jit(solution)/shard_map/all_gather | solution.py:508
  30.3 0.0 collective-permute-done.rb_ref
  30.3 0.7 %shard_map.54 = (f32[12,16,128]{2,1,0:T(8,128)S(1)}, f32[12,16,128]{2,1,0:T(8,128)S(1)}, f32[15,2,2,16,128]{4,3,2,1,0:T(8,128)S(1)}, f32[2,2,16,128]{3,2,1,0:T(8,128)S(1)}, f32[19,2,2,16,128]{4,3,2,1,0:T(8,128)S(1)}) custom-call(f32[15,2,2,16,128]{4,3,2,1,0:T(8,128)S(1)} %get-tuple-element.16.hs_ref, f32[19,2,2,16,128]{4,3,2,1,0:T(8,128)S(1)} %shard_map.53.fs_ref, ...), custom_call_target="tpu_custom_call" | custom-call | tf_op jit(solution)/shard_map/pallas_call | solution.py:490
  31.0 7.1 %collective-permute-start.1 = (f32[12,16,128]{2,1,0:T(8,128)S(1)}, f32[12,16,128]{2,1,0:T(8,128)S(1)}, u32[]{:S(2)}, u32[]{:S(2)}) collective-permute-start(f32[12,16,128]{2,1,0:T(8,128)S(1)} %get-tuple-element.25), channel_id=1, source_target_pairs={{0,760},{8,16},{16,8},{24,32},{32,24},{40,48},{48,40},{56,64},{64,... | collective-permute-start | bytes 294920 | tf_op jit(solution)/shard_map/ppermute | solution.py:518
  38.2 6.5 %all-gather.3 = f32[24,16,128]{2,1,0:T(8,128)S(1)} all-gather(f32[12,16,128]{2,1,0:T(8,128)S(1)} %get-tuple-element.24), channel_id=5, replica_groups={{0,8},{16,24},{32,40},{48,56},{64,72},{80,88},{96,104},{112,120},{128,1..., dimensions={0}, use_global_device_ids=true | all-gather | bytes 294912 | tf_op jit(solution)/shard_map/all_gather | solution.py:508
  44.7 0.0 collective-permute-done.1.rb_ref
  44.7 1.1 %shard_map.55 = (f32[15,2,16,128]{3,2,1,0:T(8,128)}, f32[19,2,16,128]{3,2,1,0:T(8,128)}) custom-call(f32[15,2,2,16,128]{4,3,2,1,0:T(8,128)S(1)} %get-tuple-element.21.hs_ref, f32[19,2,2,16,128]{4,3,2,1,0:T(8,128)S(1)} %get-tuple-element.22.f1_ref, f32[2,2,16,128]{3,2,1,0:T(8,128)S(1)} %get-tuple-element.23.sums_ref, ...), custom_call_target="tpu_custom_call" | custom-call | tf_op jit(solution)/shard_map/pallas_call | solution.py:490
  (1 shorter events, 0.0 us)
Async XLA Ops:
  0.6 1.0 %copy-start = (f32[19,2,16,128]{3,2,1,0:T(8,128)S(1)}, f32[19,2,16,128]{3,2,1,0:T(8,128)}, u32[]{:S(2)}) copy-start(f32[19,2,16,128]{3,2,1,0:T(8,128)} %f_ref.5) | copy-start | bytes 933892
  0.6 1.0 %copy-start.2 = (s32[2,16,128]{2,1,0:T(8,128)S(1)}, s32[2,16,128]{2,1,0:T(8,128)}, u32[]{:S(2)}) copy-start(s32[2,16,128]{2,1,0:T(8,128)} %s_ref.3) | copy-start | bytes 49156
  0.6 1.0 %copy-start.1 = (f32[15,2,16,128]{3,2,1,0:T(8,128)S(1)}, f32[15,2,16,128]{3,2,1,0:T(8,128)}, u32[]{:S(2)}) copy-start(f32[15,2,16,128]{3,2,1,0:T(8,128)} %h_ref.3) | copy-start | bytes 737284
  13.0 17.3 %collective-permute-start = (f32[12,16,128]{2,1,0:T(8,128)S(1)}, f32[12,16,128]{2,1,0:T(8,128)S(1)}, u32[]{:S(2)}, u32[]{:S(2)}) collective-permute-start(f32[12,16,128]{2,1,0:T(8,128)S(1)} %get-tuple-element.20), channel_id=1, source_target_pairs={{0,760},{8,16},{16,8},{24,32},{32,24},{40,48},{48,40},{56,64},{64,... | collective-permute-start | bytes 294920 | tf_op jit(solution)/shard_map/ppermute | solution.py:518
  31.0 13.6 %collective-permute-start.1 = (f32[12,16,128]{2,1,0:T(8,128)S(1)}, f32[12,16,128]{2,1,0:T(8,128)S(1)}, u32[]{:S(2)}, u32[]{:S(2)}) collective-permute-start(f32[12,16,128]{2,1,0:T(8,128)S(1)} %get-tuple-element.25), channel_id=1, source_target_pairs={{0,760},{8,16},{16,8},{24,32},{32,24},{40,48},{48,40},{56,64},{64,... | collective-permute-start | bytes 294920 | tf_op jit(solution)/shard_map/ppermute | solution.py:518

commit v6 on v5

--- a/solution.py
+++ b/solution.py
@@ -480,7 +480,7 @@
 TILE = (16, 128)
 COVER = pl.CostEstimate(flops=2_000_000_000, bytes_accessed=4_000_000, transcendentals=0)
 LIMIT = 16 * 1024 * 1024
-NEAR_Y, FAR_Y, NEAR_X, FAR_X = True, True, True, False
+NEAR_Y, FAR_Y, NEAR_X, FAR_X = True, False, True, False
 
 
 def call(kernel, outs, *args, scratch=(), sems=None, source=VMEM, target=VMEM, cost=None):

time: 46 us -> 46.1 us (level)
  the two profiles are of different devices: /device:TPU:192 before, /device:TPU:1 now
where the time goes in v6:
time: 46.1 us; the launch traced here: 45.9 us
  starting transfers between devices  24.2 us (52%)
  blocking collectives  17.1 us (37%)
  Pallas kernels  2.84 us (6%)
  local copies, waits for them, and re-layouts  1.02 us (2%)
  between operations  0.71 us (2%)
    ppermute x3, starting transfers between devices, swap_far(): return lax.ppermute(block, axis, route)  24.2 us
    all_gather x3, blocking collectives, swap_near(): return lax.all_gather(block, axis, axis_index_groups=groups)  17.1 us
    pallas_call x6, Pallas kernels, call(): pl.pallas_call(kernel, out_shape=[out if hasattr(out, 'dtype') else jax.S...  2.84 us
    unnamed x6, local copies, waits for them, and re-layouts  1.02 us
  transfers between devices with their start and end apart: 3, of which 0 were waited for; matrix products, arithmetic and copies ran while one was open for 0% of the time, Pallas kernels for 1%

profile of v6, /device:TPU:1, one launch (start us, length us, event | category | flops | bytes accessed | tf_op | source)
XLA Modules:
  0.0 45.9 jit_solution(860491438835915811)
XLA Ops:
  0.6 0.0 copy-start
  0.6 0.0 copy-start.2
  0.6 0.0 copy-start.1
  0.7 0.9 %copy-done = f32[19,2,16,128]{3,2,1,0:T(8,128)S(1)} copy-done((f32[19,2,16,128]{3,2,1,0:T(8,128)S(1)}, f32[19,2,16,128]{3,2,1,0:T(8,128)}, u32[]{:S(2)}) %copy-start) | copy-done | bytes 311320
  1.6 0.0 copy-done.2
  1.6 0.1 copy-done.1
  1.7 0.3 shard_map.51
  2.0 9.0 %collective-permute-start = (f32[3,16,128]{2,1,0:T(8,128)S(1)}, f32[3,16,128]{2,1,0:T(8,128)S(1)}, u32[]{:S(2)}, u32[]{:S(2)}) collective-permute-start(f32[3,16,128]{2,1,0:T(8,128)S(1)} %get-tuple-element.15), channel_id=1, source_target_pairs={{0,7},{1,2},{2,1},{3,4},{4,3},{5,6},{6,5},{7,0},{8,15},{9,10},{10,... | collective-permute-start | bytes 73736 | tf_op jit(solution)/shard_map/ppermute | solution.py:518
  11.0 8.0 %all-gather = f32[6,16,128]{2,1,0:T(8,128)S(1)} all-gather(f32[3,16,128]{2,1,0:T(8,128)S(1)} %get-tuple-element.14), channel_id=2, replica_groups={{0,1},{2,3},{4,5},{6,7},{8,9},{10,11},{12,13},{14,15},{16,17},{18,19},{..., dimensions={0}, use_global_device_ids=true | all-gather | bytes 73728 | tf_op jit(solution)/shard_map/all_gather | solution.py:508
  19.0 0.0 collective-permute-done.yb_ref
  19.0 0.4 shard_map.52
  19.4 9.1 %collective-permute-start.1 = (f32[12,16,128]{2,1,0:T(8,128)S(1)}, f32[12,16,128]{2,1,0:T(8,128)S(1)}, u32[]{:S(2)}, u32[]{:S(2)}) collective-permute-start(f32[12,16,128]{2,1,0:T(8,128)S(1)} %get-tuple-element.20), channel_id=1, source_target_pairs={{0,760},{8,16},{16,8},{24,32},{32,24},{40,48},{48,40},{56,64},{64,... | collective-permute-start | bytes 294920 | tf_op jit(solution)/shard_map/ppermute | solution.py:518
  28.5 0.3 shard_map.53.fs_ref
  28.8 4.4 %all-gather.1 = f32[24,16,128]{2,1,0:T(8,128)S(1)} all-gather(f32[12,16,128]{2,1,0:T(8,128)S(1)} %get-tuple-element.19), channel_id=3, replica_groups={{0,8},{16,24},{32,40},{48,56},{64,72},{80,88},{96,104},{112,120},{128,1..., dimensions={0}, use_global_device_ids=true | all-gather | bytes 294912 | tf_op jit(solution)/shard_map/all_gather | solution.py:508
  33.2 0.0 collective-permute-done.1.rb_ref
  33.2 0.7 %shard_map.54 = (f32[12,16,128]{2,1,0:T(8,128)S(1)}, f32[12,16,128]{2,1,0:T(8,128)S(1)}, f32[15,2,2,16,128]{4,3,2,1,0:T(8,128)S(1)}, f32[2,2,16,128]{3,2,1,0:T(8,128)S(1)}, f32[19,2,2,16,128]{4,3,2,1,0:T(8,128)S(1)}) custom-call(f32[15,2,2,16,128]{4,3,2,1,0:T(8,128)S(1)} %get-tuple-element.16.hs_ref, f32[19,2,2,16,128]{4,3,2,1,0:T(8,128)S(1)} %shard_map.53.fs_ref, ...), custom_call_target="tpu_custom_call" | custom-call | tf_op jit(solution)/shard_map/pallas_call | solution.py:490
  33.9 6.1 %collective-permute-start.2 = (f32[12,16,128]{2,1,0:T(8,128)S(1)}, f32[12,16,128]{2,1,0:T(8,128)S(1)}, u32[]{:S(2)}, u32[]{:S(2)}) collective-permute-start(f32[12,16,128]{2,1,0:T(8,128)S(1)} %get-tuple-element.25), channel_id=1, source_target_pairs={{0,760},{8,16},{16,8},{24,32},{32,24},{40,48},{48,40},{56,64},{64,... | collective-permute-start | bytes 294920 | tf_op jit(solution)/shard_map/ppermute | solution.py:518
  40.1 4.7 %all-gather.2 = f32[24,16,128]{2,1,0:T(8,128)S(1)} all-gather(f32[12,16,128]{2,1,0:T(8,128)S(1)} %get-tuple-element.24), channel_id=4, replica_groups={{0,8},{16,24},{32,40},{48,56},{64,72},{80,88},{96,104},{112,120},{128,1..., dimensions={0}, use_global_device_ids=true | all-gather | bytes 294912 | tf_op jit(solution)/shard_map/all_gather | solution.py:508
  44.8 0.0 collective-permute-done.2.rb_ref
  44.8 1.1 %shard_map.55 = (f32[15,2,16,128]{3,2,1,0:T(8,128)}, f32[19,2,16,128]{3,2,1,0:T(8,128)}) custom-call(f32[15,2,2,16,128]{4,3,2,1,0:T(8,128)S(1)} %get-tuple-element.21.hs_ref, f32[19,2,2,16,128]{4,3,2,1,0:T(8,128)S(1)} %get-tuple-element.22.f1_ref, f32[2,2,16,128]{3,2,1,0:T(8,128)S(1)} %get-tuple-element.23.sums_ref, ...), custom_call_target="tpu_custom_call" | custom-call | tf_op jit(solution)/shard_map/pallas_call | solution.py:490
  (1 shorter events, 0.0 us)
Async XLA Ops:
  0.6 1.0 %copy-start = (f32[19,2,16,128]{3,2,1,0:T(8,128)S(1)}, f32[19,2,16,128]{3,2,1,0:T(8,128)}, u32[]{:S(2)}) copy-start(f32[19,2,16,128]{3,2,1,0:T(8,128)} %f_ref.5) | copy-start | bytes 933892
  0.6 1.0 %copy-start.2 = (s32[2,16,128]{2,1,0:T(8,128)S(1)}, s32[2,16,128]{2,1,0:T(8,128)}, u32[]{:S(2)}) copy-start(s32[2,16,128]{2,1,0:T(8,128)} %s_ref.3) | copy-start | bytes 49156
  0.6 1.0 %copy-start.1 = (f32[15,2,16,128]{3,2,1,0:T(8,128)S(1)}, f32[15,2,16,128]{3,2,1,0:T(8,128)}, u32[]{:S(2)}) copy-start(f32[15,2,16,128]{3,2,1,0:T(8,128)} %h_ref.3) | copy-start | bytes 737284
  2.0 17.0 %collective-permute-start = (f32[3,16,128]{2,1,0:T(8,128)S(1)}, f32[3,16,128]{2,1,0:T(8,128)S(1)}, u32[]{:S(2)}, u32[]{:S(2)}) collective-permute-start(f32[3,16,128]{2,1,0:T(8,128)S(1)} %get-tuple-element.15), channel_id=1, source_target_pairs={{0,7},{1,2},{2,1},{3,4},{4,3},{5,6},{6,5},{7,0},{8,15},{9,10},{10,... | collective-permute-start | bytes 73736 | tf_op jit(solution)/shard_map/ppermute | solution.py:518
  19.4 13.8 %collective-permute-start.1 = (f32[12,16,128]{2,1,0:T(8,128)S(1)}, f32[12,16,128]{2,1,0:T(8,128)S(1)}, u32[]{:S(2)}, u32[]{:S(2)}) collective-permute-start(f32[12,16,128]{2,1,0:T(8,128)S(1)} %get-tuple-element.20), channel_id=1, source_target_pairs={{0,760},{8,16},{16,8},{24,32},{32,24},{40,48},{48,40},{56,64},{64,... | collective-permute-start | bytes 294920 | tf_op jit(solution)/shard_map/ppermute | solution.py:518
  33.9 10.8 %collective-permute-start.2 = (f32[12,16,128]{2,1,0:T(8,128)S(1)}, f32[12,16,128]{2,1,0:T(8,128)S(1)}, u32[]{:S(2)}, u32[]{:S(2)}) collective-permute-start(f32[12,16,128]{2,1,0:T(8,128)S(1)} %get-tuple-element.25), channel_id=1, source_target_pairs={{0,760},{8,16},{16,8},{24,32},{32,24},{40,48},{48,40},{56,64},{64,... | collective-permute-start | bytes 294920 | tf_op jit(solution)/shard_map/ppermute | solution.py:518
